TPU v7x, 256 devices: a whole 4x4x8 slice. The times are simulated.
256 devices in a mesh: bar: 128 (over y_lo, x, z, core), lat: 2 (over y_hi).
Axes of the slice: x: 4, y: 4 (y_hi: 2, y_lo: 2; y = y_hi * 2 + y_lo), z: 8, core: 2. Of those that a mesh axis runs over, the one named last changes fastest.
Arguments:
- displace: float32 [3, 768, 16, 128], P(None, 'bar', 'lat'), may hold values from -6 to 6
- velocity: float32 [3, 768, 16, 128], P(None, 'bar', 'lat'), may hold values from -6 to 6
- bond_low: int32 [768, 16, 128], P('bar', 'lat'), may hold values from 0 to 2147483646
- bond_high: int32 [768, 16, 128], P('bar', 'lat'), may hold values from 0 to 1073741823
- bc_type: int32 [128], replicated, may hold values from 0 to 3
Outputs:
- displace_out: float32 [3, 768, 16, 128], P(None, 'bar', 'lat')
- velocity_out: float32 [3, 768, 16, 128], P(None, 'bar', 'lat')
All inputs are finite; a program needn't handle non-finite values.
Results may differ from a plain program's by a relative error of at most 0.00002.
Values sent between devices are 32-bit elements; how exact they have to be, the bound alone decides.
A program may use at most 64 MiB of HBM per device.

v0:
```python
import jax
import jax.numpy as jnp
from jax import lax
from jax.sharding import PartitionSpec as P

STEPS = 2


modulus = 0.1
time_step = 0.5


def with_halo(cells, sides, width):
    for axis, dim in sides:
        count = lax.axis_size(axis)
        ends = count - 1
        head = lax.slice_in_dim(cells, 0, width, axis=dim)
        tail = lax.slice_in_dim(cells, cells.shape[dim] - width, cells.shape[dim], axis=dim)
        cells = jnp.concatenate(
            [
                lax.ppermute(tail, axis, [(i, (i + 1) % count) for i in range(ends)]),
                cells,
                lax.ppermute(head, axis, [((i + 1) % count, i) for i in range(ends)]),
            ],
            axis=dim,
        )
    return cells


def bond_offsets():
    found = []
    for off_x in range(-3, 4):
        for off_y in range(-3, 4):
            for off_z in range(-3, 4):
                square = off_x * off_x + off_y * off_y + off_z * off_z
                if square == 0 or square > 9:
                    continue
                if (
                    off_x > 0
                    or (off_x == 0 and off_y > 0)
                    or (off_x == 0 and off_y == 0 and (off_z > 0))
                ):
                    found.append((off_x, off_y, off_z))
    return found


def inside(coords, shift_by, total):
    moved = coords + shift_by
    return ((moved >= 0) & (moved < total)).astype(jnp.float32)


def bond_forces(moving, low_bits, high_bits, anchor_x, anchor_y, total_x, total_y):
    size_x, size_y, size_z = (moving.shape[1], moving.shape[2], moving.shape[3])
    padded = jnp.pad(moving, ((0, 0), (3, 3), (3, 3), (3, 3)))
    coord_x = anchor_x + jnp.arange(size_x, dtype=jnp.int32)
    coord_y = anchor_y + jnp.arange(size_y, dtype=jnp.int32)
    coord_z = jnp.arange(size_z, dtype=jnp.int32)
    here_x = inside(coord_x, 0, total_x)
    here_y = inside(coord_y, 0, total_y)
    force_x = jnp.zeros(moving.shape[1:], jnp.float32)
    force_y = jnp.zeros(moving.shape[1:], jnp.float32)
    force_z = jnp.zeros(moving.shape[1:], jnp.float32)
    for number, (off_x, off_y, off_z) in enumerate(bond_offsets()):
        if number < 31:
            flag_word, bit_pos = (low_bits, number)
        else:
            flag_word, bit_pos = (high_bits, number - 31)
        intact = (1 - jnp.bitwise_and(jnp.right_shift(flag_word, bit_pos), 1)).astype(jnp.float32)
        neighbour = padded[
            :,
            3 + off_x : 3 + off_x + size_x,
            3 + off_y : 3 + off_y + size_y,
            3 + off_z : 3 + off_z + size_z,
        ]
        mask_x = here_x * inside(coord_x, off_x, total_x)
        mask_y = here_y * inside(coord_y, off_y, total_y)
        mask_z = inside(coord_z, off_z, size_z)
        reach_mask = mask_x[:, None, None] * mask_y[None, :, None] * mask_z[None, None, :]
        stretch = (
            off_x * (neighbour[0] - moving[0])
            + off_y * (neighbour[1] - moving[1])
            + off_z * (neighbour[2] - moving[2])
        )
        length = float(off_x * off_x + off_y * off_y + off_z * off_z) ** 1.5
        bond_term = modulus / length * intact * reach_mask * stretch
        bond_pad = jnp.pad(bond_term, 3)
        back_term = bond_pad[
            3 - off_x : 3 - off_x + size_x,
            3 - off_y : 3 - off_y + size_y,
            3 - off_z : 3 - off_z + size_z,
        ]
        net_term = bond_term - back_term
        force_x = force_x + off_x * net_term
        force_y = force_y + off_y * net_term
        force_z = force_z + off_z * net_term
    return jnp.stack([force_x, force_y, force_z])


def plane_retain(bc_type, first_plane, count, per_slab):
    planes = first_plane + jnp.arange(count, dtype=jnp.int32)
    slabs = jnp.arange(bc_type.shape[0], dtype=jnp.int32)
    match = (planes[:, None] // per_slab == slabs[None, :]).astype(jnp.float32)
    code = jnp.sum(match * bc_type.astype(jnp.float32)[None, :], axis=1)
    return (1.0 - 0.2 * code)[None, :, None, None]


def local(displace, velocity, bond_low, bond_high, bc_type):
    size_x, size_y = (displace.shape[1], displace.shape[2])
    total_x = size_x * lax.axis_size("bar")
    total_y = size_y * lax.axis_size("lat")
    start_x = lax.axis_index("bar") * size_x
    start_y = lax.axis_index("lat") * size_y
    packed = jnp.stack([bond_low, bond_high])
    rims = with_halo(packed, (("bar", 1), ("lat", 2)), 3)
    retain = plane_retain(bc_type, start_x, size_x, size_x)
    for step_no in range(STEPS):
        wide = with_halo(displace, (("bar", 1), ("lat", 2)), 3)
        forces = bond_forces(wide, rims[0], rims[1], start_x - 3, start_y - 3, total_x, total_y)
        forces = forces[:, 3:-3, 3:-3, :]
        velocity = retain * (velocity + time_step * forces)
        displace = displace + time_step * velocity
    return (displace, velocity)


def solution(mesh):
    return jax.shard_map(
        local,
        mesh=mesh,
        in_specs=(
            P(None, "bar", "lat", None),
            P(None, "bar", "lat", None),
            P("bar", "lat", None),
            P("bar", "lat", None),
            P(),
        ),
        out_specs=(P(None, "bar", "lat", None), P(None, "bar", "lat", None)),
        check_vma=False,
    )
```

profile of v0, /device:TPU:24, one launch (start us, length us, event | category | flops | bytes accessed | tf_op | source)
XLA Modules:
  0.0 84.7 jit_solution(1490329419908658660)
XLA Ops:
  0.7 0.8 fusion.993
  1.5 1.9 %collective-permute-start.4 = (f32[3,3,8,128]{3,2,1,0:T(8,128)S(1)}, f32[3,3,8,128]{3,2,1,0:T(8,128)S(1)}, u32[]{:S(2)}, u32[]{:S(2)}) collective-permute-start(f32[3,3,8,128]{3,2,1,0:T(8,128)S(1)} %get-tuple-element.141), channel_id=1, source_target_pairs={{0,2},{2,4},{4,6},{6,8},{8,10},{10,12},{12,14},{14,16},{16,18},{18... | collective-permute-start | bytes 110600 | tf_op jit(solution)/shard_map/ppermute | solution.py:21
  3.4 9.6 %collective-permute-start.5 = (f32[3,3,8,128]{3,2,1,0:T(8,128)S(1)}, f32[3,3,8,128]{3,2,1,0:T(8,128)S(1)}, u32[]{:S(2)}, u32[]{:S(2)}) collective-permute-start(f32[3,3,8,128]{3,2,1,0:T(8,128)S(1)} %get-tuple-element.140), channel_id=1, source_target_pairs={{2,0},{4,2},{6,4},{8,6},{10,8},{12,10},{14,12},{16,14},{18,16},{20... | collective-permute-start | bytes 110600 | tf_op jit(solution)/shard_map/ppermute | solution.py:23
  13.0 0.8 fusion.986
  13.7 2.6 %collective-permute-start.1 = (s32[2,3,8,128]{3,2,1,0:T(8,128)S(1)}, s32[2,3,8,128]{3,2,1,0:T(8,128)S(1)}, u32[]{:S(2)}, u32[]{:S(2)}) collective-permute-start(s32[2,3,8,128]{3,2,1,0:T(8,128)S(1)} %get-tuple-element.143), channel_id=1, source_target_pairs={{2,0},{4,2},{6,4},{8,6},{10,8},{12,10},{14,12},{16,14},{18,16},{20... | collective-permute-start | bytes 73736 | tf_op jit(solution)/shard_map/ppermute | solution.py:23
  16.3 1.9 %collective-permute-start = (s32[2,3,8,128]{3,2,1,0:T(8,128)S(1)}, s32[2,3,8,128]{3,2,1,0:T(8,128)S(1)}, u32[]{:S(2)}, u32[]{:S(2)}) collective-permute-start(s32[2,3,8,128]{3,2,1,0:T(8,128)S(1)} %get-tuple-element.142), channel_id=1, source_target_pairs={{0,2},{2,4},{4,6},{6,8},{8,10},{10,12},{12,14},{14,16},{16,18},{18... | collective-permute-start | bytes 73736 | tf_op jit(solution)/shard_map/ppermute | solution.py:21
  18.4 0.7 convert_element_type.1109
  19.3 6.4 %collective-permute-done = s32[2,3,8,128]{3,2,1,0:T(8,128)S(1)} collective-permute-done((s32[2,3,8,128]{3,2,1,0:T(8,128)S(1)}, s32[2,3,8,128]{3,2,1,0:T(8,128)S(1)}, u32[]{:S(2)}, u32[]{:S(2)}) %collective-permute-start) | collective-permute-done | bytes 24608 | tf_op jit(solution)/shard_map/ppermute | solution.py:21
  25.8 2.7 %collective-permute-start.3 = (s32[2,12,3,128]{3,2,1,0:T(4,128)S(1)}, s32[2,12,3,128]{3,2,1,0:T(4,128)S(1)}, u32[]{:S(2)}, u32[]{:S(2)}) collective-permute-start(s32[2,12,3,128]{3,2,1,0:T(4,128)S(1)} %get-tuple-element.137), channel_id=1, source_target_pairs={{1,0},{3,2},{5,4},{7,6},{9,8},{11,10},{13,12},{15,14},{17,16},{19,... | collective-permute-start | bytes 110600 | tf_op jit(solution)/shard_map/ppermute | solution.py:23
  28.6 1.3 %collective-permute-start.2 = (s32[2,12,3,128]{3,2,1,0:T(4,128)S(1)}, s32[2,12,3,128]{3,2,1,0:T(4,128)S(1)}, u32[]{:S(2)}, u32[]{:S(2)}) collective-permute-start(s32[2,12,3,128]{3,2,1,0:T(4,128)S(1)} %get-tuple-element.136), channel_id=1, source_target_pairs={{0,1},{2,3},{4,5},{6,7},{8,9},{10,11},{12,13},{14,15},{16,17},{18,... | collective-permute-start | bytes 110600 | tf_op jit(solution)/shard_map/ppermute | solution.py:21
  30.0 6.1 %collective-permute-start.7 = (f32[3,12,3,128]{3,2,1,0:T(4,128)S(1)}, f32[3,12,3,128]{3,2,1,0:T(4,128)S(1)}, u32[]{:S(2)}, u32[]{:S(2)}) collective-permute-start(f32[3,12,3,128]{3,2,1,0:T(4,128)S(1)} %get-tuple-element.135), channel_id=1, source_target_pairs={{1,0},{3,2},{5,4},{7,6},{9,8},{11,10},{13,12},{15,14},{17,16},{19,... | collective-permute-start | bytes 165896 | tf_op jit(solution)/shard_map/ppermute | solution.py:23
  36.0 1.3 %collective-permute-start.6 = (f32[3,12,3,128]{3,2,1,0:T(4,128)S(1)}, f32[3,12,3,128]{3,2,1,0:T(4,128)S(1)}, u32[]{:S(2)}, u32[]{:S(2)}) collective-permute-start(f32[3,12,3,128]{3,2,1,0:T(4,128)S(1)} %get-tuple-element.134), channel_id=1, source_target_pairs={{0,1},{2,3},{4,5},{6,7},{8,9},{10,11},{12,13},{14,15},{16,17},{18,... | collective-permute-start | bytes 165896 | tf_op jit(solution)/shard_map/ppermute | solution.py:21
  37.4 0.6 collective-permute-done.7
  38.0 5.8 %collective-permute-done.6 = f32[3,12,3,128]{3,2,1,0:T(4,128)S(1)} collective-permute-done((f32[3,12,3,128]{3,2,1,0:T(4,128)S(1)}, f32[3,12,3,128]{3,2,1,0:T(4,128)S(1)}, u32[]{:S(2)}, u32[]{:S(2)}) %collective-permute-start.6) | collective-permute-done | bytes 55328 | tf_op jit(solution)/shard_map/ppermute | solution.py:21
  44.3 0.2 bitcast_multiply_fusion.77
  45.0 0.2 bitcast_multiply_fusion.97
  45.3 0.2 bitcast_multiply_fusion.107
  45.5 0.2 bitcast_multiply_fusion.113
  45.8 0.2 bitcast_multiply_fusion.117
  46.0 0.2 bitcast_multiply_fusion.123
  46.2 0.2 bitcast_multiply_fusion.127
  46.5 0.2 bitcast_multiply_fusion.133
  46.7 0.2 bitcast_multiply_fusion.137
  47.0 0.2 bitcast_multiply_fusion.143
  47.2 0.2 bitcast_multiply_fusion.147
  47.5 0.2 bitcast_multiply_fusion.153
  47.7 0.2 bitcast_multiply_fusion.159
  48.0 0.3 bitcast_multiply_fusion.165
  48.3 0.3 bitcast_multiply_fusion.175
  48.5 0.2 bitcast_multiply_fusion.173
  49.0 0.2 bitcast_multiply_fusion.103
  49.2 0.3 bitcast_multiply_fusion.181
  49.7 1.2 %add_bitcast_fusion.3 = f32[1,12,14,128]{3,2,1,0:T(8,128)S(1)} fusion(f32[12,14,128]{2,1,0:T(8,128)S(1)} %get-tuple-element.127, f32[12,14,128]{2,1,0:T(8,128)S(1)} %get-tuple-element.126, f32[12,14,128]{2,1,0:T(8,128)S(1)} %get-tuple-element.125, f32[12,14,128]{2,1,0:T(8,128)S(1)} %get-tuple-element.131, f32[12,14,128]{2,1,0:T(8,128)S(1)} %get-tuple-element.124, ...), kind=kLoop, calls=%fused_computation.1661 | loop fusion | flops 3634176 | bytes 5332992 | tf_op jit(solution)/shard_map/stack | solution.py:96
  51.0 1.2 %add_bitcast_fusion.5 = (f32[1,12,14,128]{3,2,1,0:T(8,128)S(1)}, f32[12,14,128]{2,1,0:T(8,128)S(1)}) fusion(f32[12,14,128]{2,1,0:T(8,128)S(1)} %get-tuple-element.131, f32[12,14,128]{2,1,0:T(8,128)S(1)} %get-tuple-element.124, f32[12,14,128]{2,1,0:T(8,128)S(1)} %get-tuple-element.123, f32[12,14,128]{2,1,0:T(8,128)S(1)} %get-tuple-element.122, ...), kind=kLoop, calls=%fused_computation.1663 | loop fusion | flops 3333120 | bytes 5419008 | tf_op jit(solution)/shard_map/stack | solution.py:96
  52.2 1.1 %add_bitcast_fusion.4 = f32[1,12,14,128]{3,2,1,0:T(8,128)S(1)} fusion(f32[12,14,128]{2,1,0:T(8,128)S(1)} %get-tuple-element.9, f32[12,14,128]{2,1,0:T(8,128)S(1)} %get-tuple-element.131, f32[12,14,128]{2,1,0:T(8,128)S(1)} %get-tuple-element.124, f32[12,14,128]{2,1,0:T(8,128)S(1)} %get-tuple-element.123, f32[12,14,128]{2,1,0:T(8,128)S(1)} %get-tuple-element.122, ...), kind=kLoop, calls=%fused_computation.1662 | loop fusion | flops 3419136 | bytes 5160960 | tf_op jit(solution)/shard_map/stack | solution.py:96
  53.5 1.9 %collective-permute-start.9 = (f32[3,3,8,128]{3,2,1,0:T(8,128)S(1)}, f32[3,3,8,128]{3,2,1,0:T(8,128)S(1)}, u32[]{:S(2)}, u32[]{:S(2)}) collective-permute-start(f32[3,3,8,128]{3,2,1,0:T(8,128)S(1)} %get-tuple-element.139), channel_id=1, source_target_pairs={{2,0},{4,2},{6,4},{8,6},{10,8},{12,10},{14,12},{16,14},{18,16},{20... | collective-permute-start | bytes 110600 | tf_op jit(solution)/shard_map/ppermute | solution.py:23
  55.4 2.4 %collective-permute-start.8 = (f32[3,3,8,128]{3,2,1,0:T(8,128)S(1)}, f32[3,3,8,128]{3,2,1,0:T(8,128)S(1)}, u32[]{:S(2)}, u32[]{:S(2)}) collective-permute-start(f32[3,3,8,128]{3,2,1,0:T(8,128)S(1)} %get-tuple-element.138), channel_id=1, source_target_pairs={{0,2},{2,4},{4,6},{6,8},{8,10},{10,12},{12,14},{14,16},{16,18},{18... | collective-permute-start | bytes 110600 | tf_op jit(solution)/shard_map/ppermute | solution.py:21
  57.8 7.1 %collective-permute-done.8 = f32[3,3,8,128]{3,2,1,0:T(8,128)S(1)} collective-permute-done((f32[3,3,8,128]{3,2,1,0:T(8,128)S(1)}, f32[3,3,8,128]{3,2,1,0:T(8,128)S(1)}, u32[]{:S(2)}, u32[]{:S(2)}) %collective-permute-start.8) | collective-permute-done | bytes 36896 | tf_op jit(solution)/shard_map/ppermute | solution.py:21
  65.0 1.6 %collective-permute-start.11 = (f32[3,12,3,128]{3,2,1,0:T(4,128)S(1)}, f32[3,12,3,128]{3,2,1,0:T(4,128)S(1)}, u32[]{:S(2)}, u32[]{:S(2)}) collective-permute-start(f32[3,12,3,128]{3,2,1,0:T(4,128)S(1)} %get-tuple-element.133), channel_id=1, source_target_pairs={{1,0},{3,2},{5,4},{7,6},{9,8},{11,10},{13,12},{15,14},{17,16},{19,... | collective-permute-start | bytes 165896 | tf_op jit(solution)/shard_map/ppermute | solution.py:23
  66.5 1.5 %collective-permute-start.10 = (f32[3,12,3,128]{3,2,1,0:T(4,128)S(1)}, f32[3,12,3,128]{3,2,1,0:T(4,128)S(1)}, u32[]{:S(2)}, u32[]{:S(2)}) collective-permute-start(f32[3,12,3,128]{3,2,1,0:T(4,128)S(1)} %get-tuple-element.132), channel_id=1, source_target_pairs={{0,1},{2,3},{4,5},{6,7},{8,9},{10,11},{12,13},{14,15},{16,17},{18,... | collective-permute-start | bytes 165896 | tf_op jit(solution)/shard_map/ppermute | solution.py:21
  68.0 0.5 collective-permute-done.11
  68.5 5.8 %collective-permute-done.10 = f32[3,12,3,128]{3,2,1,0:T(4,128)S(1)} collective-permute-done((f32[3,12,3,128]{3,2,1,0:T(4,128)S(1)}, f32[3,12,3,128]{3,2,1,0:T(4,128)S(1)}, u32[]{:S(2)}, u32[]{:S(2)}) %collective-permute-start.10) | collective-permute-done | bytes 55328 | tf_op jit(solution)/shard_map/ppermute | solution.py:21
  74.3 0.3 bitcast_multiply_fusion.60
  75.3 0.2 bitcast_multiply_fusion.8
  76.2 0.2 bitcast_multiply_fusion.18
  76.5 0.2 bitcast_multiply_fusion.21
  76.7 0.2 bitcast_multiply_fusion.23
  76.9 0.2 bitcast_multiply_fusion.26
  77.2 0.2 bitcast_multiply_fusion.28
  77.4 0.2 bitcast_multiply_fusion.31
  77.7 0.2 bitcast_multiply_fusion.33
  77.9 0.2 bitcast_multiply_fusion.36
  78.2 0.2 bitcast_multiply_fusion.38
  78.4 0.2 bitcast_multiply_fusion.41
  78.7 0.2 bitcast_multiply_fusion.43
  78.9 0.2 bitcast_multiply_fusion.46
  79.2 0.2 bitcast_multiply_fusion.49
  79.4 0.3 bitcast_multiply_fusion.52
  79.7 0.3 bitcast_multiply_fusion.57
  80.0 0.2 bitcast_multiply_fusion.56
  80.2 1.3 %add_bitcast_fusion = f32[1,12,14,128]{3,2,1,0:T(8,128)S(1)} fusion(f32[12,14,128]{2,1,0:T(8,128)S(1)} %get-tuple-element.68, f32[12,14,128]{2,1,0:T(8,128)S(1)} %get-tuple-element.67, f32[12,14,128]{2,1,0:T(8,128)S(1)} %get-tuple-element.66, f32[12,14,128]{2,1,0:T(8,128)S(1)} %get-tuple-element.129, f32[12,14,128]{2,1,0:T(8,128)S(1)} %get-tuple-element.65, ...), kind=kLoop, calls=%fused_computation.1658 | loop fusion | flops 3634176 | bytes 5332992 | tf_op jit(solution)/shard_map/stack | solution.py:96
  81.5 1.3 %add_bitcast_fusion.2 = (f32[1,12,14,128]{3,2,1,0:T(8,128)S(1)}, f32[12,14,128]{2,1,0:T(8,128)S(1)}) fusion(f32[12,14,128]{2,1,0:T(8,128)S(1)} %get-tuple-element.129, f32[12,14,128]{2,1,0:T(8,128)S(1)} %get-tuple-element.65, f32[12,14,128]{2,1,0:T(8,128)S(1)} %get-tuple-element.64, f32[12,14,128]{2,1,0:T(8,128)S(1)} %get-tuple-element.63, ...), kind=kLoop, calls=%fused_computation.1660 | loop fusion | flops 3333120 | bytes 5419008 | tf_op jit(solution)/shard_map/stack | solution.py:96
  82.7 1.2 %add_bitcast_fusion.1 = f32[1,12,14,128]{3,2,1,0:T(8,128)S(1)} fusion(f32[12,14,128]{2,1,0:T(8,128)S(1)} %get-tuple-element.5, f32[12,14,128]{2,1,0:T(8,128)S(1)} %get-tuple-element.129, f32[12,14,128]{2,1,0:T(8,128)S(1)} %get-tuple-element.65, f32[12,14,128]{2,1,0:T(8,128)S(1)} %get-tuple-element.64, f32[12,14,128]{2,1,0:T(8,128)S(1)} %get-tuple-element.63, ...), kind=kLoop, calls=%fused_computation.1659 | loop fusion | flops 3419136 | bytes 5160960 | tf_op jit(solution)/shard_map/stack | solution.py:96
  83.9 0.7 multiply_add_fusion
  (52 shorter events, 3.3 us)
Async XLA Ops:
  0.6 25.1 %copy-start.1 = (s32[6,8,128]{2,1,0:T(8,128)S(1)}, s32[6,8,128]{2,1,0:T(8,128)}, u32[]{:S(2)}) copy-start(s32[6,8,128]{2,1,0:T(8,128)} %param.7) | copy-start | bytes 73732
  0.6 25.1 %copy-start.2 = (s32[6,8,128]{2,1,0:T(8,128)S(1)}, s32[6,8,128]{2,1,0:T(8,128)}, u32[]{:S(2)}) copy-start(s32[6,8,128]{2,1,0:T(8,128)} %param.8) | copy-start | bytes 73732
  1.5 28.4 %collective-permute-start.4 = (f32[3,3,8,128]{3,2,1,0:T(8,128)S(1)}, f32[3,3,8,128]{3,2,1,0:T(8,128)S(1)}, u32[]{:S(2)}, u32[]{:S(2)}) collective-permute-start(f32[3,3,8,128]{3,2,1,0:T(8,128)S(1)} %get-tuple-element.141), channel_id=1, source_target_pairs={{0,2},{2,4},{4,6},{6,8},{8,10},{10,12},{12,14},{14,16},{16,18},{18... | collective-permute-start | bytes 110600 | tf_op jit(solution)/shard_map/ppermute | solution.py:21
  3.4 26.5 %collective-permute-start.5 = (f32[3,3,8,128]{3,2,1,0:T(8,128)S(1)}, f32[3,3,8,128]{3,2,1,0:T(8,128)S(1)}, u32[]{:S(2)}, u32[]{:S(2)}) collective-permute-start(f32[3,3,8,128]{3,2,1,0:T(8,128)S(1)} %get-tuple-element.140), channel_id=1, source_target_pairs={{2,0},{4,2},{6,4},{8,6},{10,8},{12,10},{14,12},{16,14},{18,16},{20... | collective-permute-start | bytes 110600 | tf_op jit(solution)/shard_map/ppermute | solution.py:23
  13.7 5.6 %collective-permute-start.1 = (s32[2,3,8,128]{3,2,1,0:T(8,128)S(1)}, s32[2,3,8,128]{3,2,1,0:T(8,128)S(1)}, u32[]{:S(2)}, u32[]{:S(2)}) collective-permute-start(s32[2,3,8,128]{3,2,1,0:T(8,128)S(1)} %get-tuple-element.143), channel_id=1, source_target_pairs={{2,0},{4,2},{6,4},{8,6},{10,8},{12,10},{14,12},{16,14},{18,16},{20... | collective-permute-start | bytes 73736 | tf_op jit(solution)/shard_map/ppermute | solution.py:23
  16.3 9.5 %collective-permute-start = (s32[2,3,8,128]{3,2,1,0:T(8,128)S(1)}, s32[2,3,8,128]{3,2,1,0:T(8,128)S(1)}, u32[]{:S(2)}, u32[]{:S(2)}) collective-permute-start(s32[2,3,8,128]{3,2,1,0:T(8,128)S(1)} %get-tuple-element.142), channel_id=1, source_target_pairs={{0,2},{2,4},{4,6},{6,8},{8,10},{10,12},{12,14},{14,16},{16,18},{18... | collective-permute-start | bytes 73736 | tf_op jit(solution)/shard_map/ppermute | solution.py:21
  19.2 10.7 %copy-start = (f32[3,6,8,128]{3,2,1,0:T(8,128)S(1)}, f32[3,6,8,128]{3,2,1,0:T(8,128)}, u32[]{:S(2)}) copy-start(f32[3,6,8,128]{3,2,1,0:T(8,128)} %param.5) | copy-start | bytes 221188
  25.8 11.5 %collective-permute-start.3 = (s32[2,12,3,128]{3,2,1,0:T(4,128)S(1)}, s32[2,12,3,128]{3,2,1,0:T(4,128)S(1)}, u32[]{:S(2)}, u32[]{:S(2)}) collective-permute-start(s32[2,12,3,128]{3,2,1,0:T(4,128)S(1)} %get-tuple-element.137), channel_id=1, source_target_pairs={{1,0},{3,2},{5,4},{7,6},{9,8},{11,10},{13,12},{15,14},{17,16},{19,... | collective-permute-start | bytes 110600 | tf_op jit(solution)/shard_map/ppermute | solution.py:23
  28.6 8.8 %collective-permute-start.2 = (s32[2,12,3,128]{3,2,1,0:T(4,128)S(1)}, s32[2,12,3,128]{3,2,1,0:T(4,128)S(1)}, u32[]{:S(2)}, u32[]{:S(2)}) collective-permute-start(s32[2,12,3,128]{3,2,1,0:T(4,128)S(1)} %get-tuple-element.136), channel_id=1, source_target_pairs={{0,1},{2,3},{4,5},{6,7},{8,9},{10,11},{12,13},{14,15},{16,17},{18,... | collective-permute-start | bytes 110600 | tf_op jit(solution)/shard_map/ppermute | solution.py:21
  30.0 8.0 %collective-permute-start.7 = (f32[3,12,3,128]{3,2,1,0:T(4,128)S(1)}, f32[3,12,3,128]{3,2,1,0:T(4,128)S(1)}, u32[]{:S(2)}, u32[]{:S(2)}) collective-permute-start(f32[3,12,3,128]{3,2,1,0:T(4,128)S(1)} %get-tuple-element.135), channel_id=1, source_target_pairs={{1,0},{3,2},{5,4},{7,6},{9,8},{11,10},{13,12},{15,14},{17,16},{19,... | collective-permute-start | bytes 165896 | tf_op jit(solution)/shard_map/ppermute | solution.py:23
  36.0 7.8 %collective-permute-start.6 = (f32[3,12,3,128]{3,2,1,0:T(4,128)S(1)}, f32[3,12,3,128]{3,2,1,0:T(4,128)S(1)}, u32[]{:S(2)}, u32[]{:S(2)}) collective-permute-start(f32[3,12,3,128]{3,2,1,0:T(4,128)S(1)} %get-tuple-element.134), channel_id=1, source_target_pairs={{0,1},{2,3},{4,5},{6,7},{8,9},{10,11},{12,13},{14,15},{16,17},{18,... | collective-permute-start | bytes 165896 | tf_op jit(solution)/shard_map/ppermute | solution.py:21
  52.2 1.2 %copy-start.3 = (f32[3,6,8,128]{3,2,1,0:T(8,128)S(1)}, f32[3,6,8,128]{3,2,1,0:T(8,128)}, u32[]{:S(2)}) copy-start(f32[3,6,8,128]{3,2,1,0:T(8,128)} %param.6) | copy-start | bytes 221188
  53.5 4.3 %collective-permute-start.9 = (f32[3,3,8,128]{3,2,1,0:T(8,128)S(1)}, f32[3,3,8,128]{3,2,1,0:T(8,128)S(1)}, u32[]{:S(2)}, u32[]{:S(2)}) collective-permute-start(f32[3,3,8,128]{3,2,1,0:T(8,128)S(1)} %get-tuple-element.139), channel_id=1, source_target_pairs={{2,0},{4,2},{6,4},{8,6},{10,8},{12,10},{14,12},{16,14},{18,16},{20... | collective-permute-start | bytes 110600 | tf_op jit(solution)/shard_map/ppermute | solution.py:23
  55.4 9.5 %collective-permute-start.8 = (f32[3,3,8,128]{3,2,1,0:T(8,128)S(1)}, f32[3,3,8,128]{3,2,1,0:T(8,128)S(1)}, u32[]{:S(2)}, u32[]{:S(2)}) collective-permute-start(f32[3,3,8,128]{3,2,1,0:T(8,128)S(1)} %get-tuple-element.138), channel_id=1, source_target_pairs={{0,2},{2,4},{4,6},{6,8},{8,10},{10,12},{12,14},{14,16},{16,18},{18... | collective-permute-start | bytes 110600 | tf_op jit(solution)/shard_map/ppermute | solution.py:21
  65.0 3.5 %collective-permute-start.11 = (f32[3,12,3,128]{3,2,1,0:T(4,128)S(1)}, f32[3,12,3,128]{3,2,1,0:T(4,128)S(1)}, u32[]{:S(2)}, u32[]{:S(2)}) collective-permute-start(f32[3,12,3,128]{3,2,1,0:T(4,128)S(1)} %get-tuple-element.133), channel_id=1, source_target_pairs={{1,0},{3,2},{5,4},{7,6},{9,8},{11,10},{13,12},{15,14},{17,16},{19,... | collective-permute-start | bytes 165896 | tf_op jit(solution)/shard_map/ppermute | solution.py:23
  66.5 7.8 %collective-permute-start.10 = (f32[3,12,3,128]{3,2,1,0:T(4,128)S(1)}, f32[3,12,3,128]{3,2,1,0:T(4,128)S(1)}, u32[]{:S(2)}, u32[]{:S(2)}) collective-permute-start(f32[3,12,3,128]{3,2,1,0:T(4,128)S(1)} %get-tuple-element.132), channel_id=1, source_target_pairs={{0,1},{2,3},{4,5},{6,7},{8,9},{10,11},{12,13},{14,15},{16,17},{18,... | collective-permute-start | bytes 165896 | tf_op jit(solution)/shard_map/ppermute | solution.py:21
where the time goes:
time: 85.2 us; the launch traced here: 84.7 us
  starting transfers between devices  34.7 us (41%)
  waiting for transfers between devices  26.2 us (31%)
  other arithmetic  21.5 us (25%)
  between operations  1.35 us (2%)
  local copies, waits for them, and re-layouts  0.92 us (1%)
    ppermute x6, waiting for transfers between devices, with_halo(): lax.ppermute(tail, axis, [(i, (i + 1) % count) for i in range(ends)])  25.1 us
    ppermute x6, starting transfers between devices, with_halo(): lax.ppermute(head, axis, [((i + 1) % count, i) for i in range(ends)])  24.4 us
    mul x48, other arithmetic, bond_forces(): bond_term = modulus / length * intact * reach_mask * stretch  11.4 us
    ppermute x6, starting transfers between devices, with_halo(): lax.ppermute(tail, axis, [(i, (i + 1) % count) for i in range(ends)])  10.3 us
    another operation x6, other arithmetic, bond_forces(): return jnp.stack([force_x, force_y, force_z])  7.31 us
  transfers between devices with their start and end apart: 12, of which 6 were waited for; matrix products, arithmetic and copies ran while one was open for 2% of the time, Pallas kernels for 0%

commit v1 on v0

v1 whole, which is shorter than its diff:
```python
import functools

import jax
import jax.numpy as jnp
from jax import lax
from jax.experimental import pallas as pl
from jax.experimental.pallas import tpu as pltpu
from jax.sharding import PartitionSpec as P

STEPS = 2
modulus = 0.1
time_step = 0.5
MESH = pl.DeviceIdType.MESH

CX, RY, NZ = 6, 8, 128
PLANES, ROWS = CX + 6, 3 * RY
X0, Y0 = 3, RY


def bond_offsets():
    found = []
    for a in range(-3, 4):
        for b in range(-3, 4):
            for c in range(-3, 4):
                square = a * a + b * b + c * c
                if square == 0 or square > 9:
                    continue
                if a > 0 or (a == 0 and b > 0) or (a == 0 and b == 0 and c > 0):
                    found.append((a, b, c))
    return found


BONDS = bond_offsets()
NUMBER = {xi: k for k, xi in enumerate(BONDS)}


def disc(b):
    return [
        (a, c)
        for c in range(-3, 4)
        for a in range(-3, 4)
        if a * a + b * b + c * c <= 9
    ]


PLACE = {abs(b): {ac: n for n, ac in enumerate(disc(b))} for b in range(4)}
SHIFTS = (-3, -2, -1, 0, 1, 2, 3)


def reach(b, c):
    return max(a for a in range(4) if a * a + b * b + c * c <= 9)


def strength(a, b, c):
    return time_step * (modulus / float(a * a + b * b + c * c) ** 1.5)


def copies(step, side, refs, sems, bar, lat):
    frame, flags = refs
    send, recv = sems
    own = slice(Y0, Y0 + RY)
    if side == 0:
        near2, far1, to2, to1 = slice(14, 16), slice(13, 14), slice(6, 8), slice(5, 6)
    else:
        near2, far1, to2, to1 = slice(8, 10), slice(10, 11), slice(16, 18), slice(18, 19)
    u = frame.at[step]
    plan = {
        "right": [
            (u.at[:, 7:9, own], u.at[:, 1:3, own]),
            (u.at[0, 6, own], u.at[0, 0, own]),
        ],
        "left": [
            (u.at[:, 3:5, own], u.at[:, 9:11, own]),
            (u.at[0, 5, own], u.at[0, 11, own]),
        ],
        "over": [
            (u.at[:, 3:9, near2], u.at[:, 3:9, to2]),
            (u.at[1, 3:9, far1], u.at[1, 3:9, to1]),
        ],
        "over_right": [(u.at[:, 7:9, near2], u.at[:, 1:3, to2])],
        "over_left": [(u.at[:, 3:5, near2], u.at[:, 9:11, to2])],
    }
    if step == 0:
        plan["right"] += [
            (flags.at[0, 8, own], flags.at[0, 2, own]),
            (flags.at[1, 6:9, own], flags.at[1, 0:3, own]),
        ]
        plan["over"] += [(flags.at[:, 3:9, near2], flags.at[:, 3:9, to2])]
        if side == 0:
            plan["over"] += [(flags.at[0, 3:9, far1], flags.at[0, 3:9, to1])]
        plan["over_right"] += [(flags.at[:, 7:9, near2], flags.at[:, 1:3, to2])]
    partner = {
        "right": (bar + 1, lat),
        "left": (bar - 1, lat),
        "over": (bar, 1 - lat),
        "over_right": (bar + 1, 1 - lat),
        "over_left": (bar - 1, 1 - lat),
    }
    made = {}
    slot = 0
    for name, pairs in plan.items():
        made[name] = []
        for src, dst in pairs:
            made[name].append(
                pltpu.make_async_remote_copy(
                    src_ref=src,
                    dst_ref=dst,
                    send_sem=send.at[step, slot],
                    recv_sem=recv.at[step, slot],
                    device_id={"bar": partner[name][0], "lat": partner[name][1]},
                    device_id_type=MESH,
                )
            )
            slot += 1
    return made


def kernel(
    bars,
    u_hbm, v_hbm, low_hbm, high_hbm, bc_hbm,
    u_out, v_out,
    frame, flags, vel, bc, turned, spun, weight, local, send, recv,
):
    bar, lat = lax.axis_index("bar"), lax.axis_index("lat")
    has_left, has_right = bar > 0, bar < bars - 1

    own_rows = slice(Y0, Y0 + RY)
    loads = [
        pltpu.make_async_copy(u_hbm, frame.at[0, :, X0:X0 + CX, own_rows], local.at[0]),
        pltpu.make_async_copy(low_hbm, flags.at[0, X0:X0 + CX, own_rows], local.at[1]),
        pltpu.make_async_copy(high_hbm, flags.at[1, X0:X0 + CX, own_rows], local.at[2]),
        pltpu.make_async_copy(v_hbm, vel, local.at[3]),
        pltpu.make_async_copy(bc_hbm, bc, local.at[4]),
    ]
    barrier = pltpu.get_barrier_semaphore()

    def greet(b, l):
        pl.semaphore_signal(barrier, inc=1, device_id={"bar": b, "lat": l}, device_id_type=MESH)

    greet(bar, 1 - lat)

    @pl.when(has_left)
    def _():
        greet(bar - 1, lat)
        greet(bar - 1, 1 - lat)

    @pl.when(has_right)
    def _():
        greet(bar + 1, lat)
        greet(bar + 1, 1 - lat)

    for copy in loads:
        copy.start()

    void = pl.multiple_of(lat * (2 * RY), RY)
    halo = pl.multiple_of((1 - lat) * (2 * RY), RY)
    zero = jnp.zeros((10, RY, NZ), jnp.float32)
    for step in range(STEPS):
        frame[step, 0, 1:11, pl.ds(void, RY), :] = zero
        for c in (-2, -1, 0, 1, 2):
            for comp in range(3):
                if c == 0 and comp != 1:
                    continue
                turned[step, c + 2, comp, 1:11, pl.ds(void, RY), :] = zero

    @pl.when(jnp.logical_not(has_left))
    def _():
        for step in range(STEPS):
            for comp in range(3):
                frame[step, comp, 0:3] = jnp.zeros((3, ROWS, NZ), jnp.float32)

    @pl.when(jnp.logical_not(has_right))
    def _():
        for step in range(STEPS):
            for comp in range(3):
                frame[step, comp, 9:12] = jnp.zeros((3, ROWS, NZ), jnp.float32)

    sems = (send, recv)
    refs = (frame, flags)

    def exchange(step, act):
        for side in range(2):
            made = copies(step, side, refs, sems, bar, lat)

            @pl.when((lat == side) if act == "start" else (lat != side))
            def _():
                for copy in made["over"]:
                    copy.start() if act == "start" else copy.wait_recv()

            for name in ("right", "left", "over_right", "over_left"):
                going_right = name.endswith("right")
                if act == "start":
                    here = has_right if going_right else has_left
                    mine = lat == side
                else:
                    here = has_left if going_right else has_right
                    mine = (lat == side) if name in ("right", "left") else (lat != side)

                @pl.when(jnp.logical_and(here, mine))
                def _():
                    for copy in made[name]:
                        copy.start() if act == "start" else copy.wait_recv()

    def drain(step):
        for side in range(2):
            made = copies(step, side, refs, sems, bar, lat)

            @pl.when(lat == side)
            def _():
                for copy in made["over"]:
                    copy.wait_send()

            for name in ("right", "left", "over_right", "over_left"):

                @pl.when(jnp.logical_and(lat == side, has_right if name.endswith("right") else has_left))
                def _():
                    for copy in made[name]:
                        copy.wait_send()

    for copy in loads[:3]:
        copy.wait()
    pl.semaphore_wait(barrier, 1 + 2 * has_left.astype(jnp.int32) + 2 * has_right.astype(jnp.int32))
    exchange(0, "start")
    for copy in loads[3:]:
        copy.wait()

    sign = 1 - 2 * lat
    fsign = sign.astype(jnp.float32)
    left_there = has_left.astype(jnp.float32)
    right_there = has_right.astype(jnp.float32)
    row = lax.broadcasted_iota(jnp.int32, (RY, NZ), 0) + lat * RY
    lane = lax.broadcasted_iota(jnp.int32, (RY, NZ), 1)

    def bound(a, b, c):
        ok = None
        if b:
            ok = (row + b >= 0) & (row + b < 2 * RY)
        if c:
            side = (lane + c >= 0) & (lane + c < NZ)
            ok = side if ok is None else ok & side
        value = strength(a, b, c)
        if ok is None:
            return jnp.full((RY, NZ), value, jnp.float32)
        return jnp.where(ok, jnp.float32(value), jnp.float32(0.0))

    def put_weight(xi, back, planes):
        a, b, c = xi
        k = NUMBER[xi]
        word, bit = (0, k) if k < 31 else (1, k - 31)
        if back:
            kept = bound(-a, -b, -c)
            a1, b1, c1 = -a, -b, -c
        else:
            kept = bound(a, b, c)
            a1, b1, c1 = a, b, c
        crossing = kept * (left_there if a1 < 0 else right_there) if a1 else kept
        place = PLACE[abs(b1)][(a1, c1)]
        for x in planes:
            if not back:
                held = flags[word, X0 + x, Y0:Y0 + RY, :]
            elif c == 0:
                held = flags[word, X0 + x - a, Y0 - b:Y0 - b + RY, :]
            else:
                held = spun[word, c + 2, X0 + x - a, Y0 - b:Y0 - b + RY, :]
            inside = 0 <= x + a1 < CX
            weight[b1 + 3, place, x] = jnp.where(
                (held & jnp.int32(1 << bit)) == 0, kept if inside else crossing, jnp.float32(0.0)
            )

    def spin(word, plane, start):
        held = flags[word, plane, pl.ds(start, RY), :]
        for c in (-2, -1, 1, 2):
            spun[word, c + 2, plane, pl.ds(start, RY), :] = pltpu.roll(held, c % NZ, axis=1)

    for x in range(CX):
        spin(0, X0 + x, Y0)
        spin(1, X0 + x, Y0)
    for x in range(CX):
        spun[0, 5, X0 + x, Y0:Y0 + RY, :] = pltpu.roll(flags[0, X0 + x, Y0:Y0 + RY, :], 3, axis=1)
    for xi in BONDS:
        put_weight(xi, False, range(CX))
    for xi in BONDS:
        if xi[1] == 0:
            put_weight(xi, True, range(xi[0], CX))
    for side in range(2):

        @pl.when(lat == side)
        def _():
            for xi in BONDS:
                if xi[1] * (1 - 2 * side) > 0:
                    put_weight(xi, True, range(xi[0], CX))

    def weights_of_halo():
        for plane in range(1, 9):
            for word in range(2):
                if plane > 2 or (word == 1 or plane == 2):
                    spin(word, plane, halo)
                    if plane < 3:
                        spin(word, plane, Y0)
        for xi in BONDS:
            if xi[1] == 0:
                put_weight(xi, True, range(min(xi[0], CX)))
        for side in range(2):

            @pl.when(lat == side)
            def _():
                for xi in BONDS:
                    if xi[1] * (1 - 2 * side) > 0:
                        put_weight(xi, True, range(xi[0]))
                    elif xi[1]:
                        put_weight(xi, True, range(CX))

    def turn(step, plane, start):
        rows = pl.ds(start, RY)
        for comp in range(3):
            held = frame[step, comp, plane, rows, :]
            if comp == 1:
                held = held * fsign
                turned[step, 2, 1, plane, rows, :] = held
            for c in (-2, -1, 1, 2):
                moved = pltpu.roll(held, (-c) % NZ, axis=1)
                turned[step, c + 2, comp, plane, rows, :] = moved * jnp.float32(c) if comp == 2 and c != 1 else moved

    def block(step, beta, c, force, part):
        far = reach(beta, c)
        start = Y0 + sign * beta if beta else Y0
        rows = pl.ds(start, RY)
        places = PLACE[abs(beta)]
        table = weight.at[3 + sign * beta] if beta else weight.at[3]

        def wanted(a, x):
            local = 0 <= x + a < CX
            if beta > 0:
                return part == "halo"
            return local == (part == "own")

        def nearby(plane):
            if c in (-3, 3):
                return far3[c][plane - X0]
            out = None
            if beta:
                out = turned[step, c + 2, 1, plane, rows, :]
                if abs(beta) != 1:
                    out = out * jnp.float32(abs(beta))
                if beta < 0:
                    out = -out if not c else out
            if c:
                second = turned[step, c + 2, 2, plane, rows, :]
                if out is None:
                    out = second
                else:
                    out = second + out if beta > 0 else second - out
            return out

        def first(plane):
            if c == 0:
                return frame[step, 0, plane, rows, :]
            return turned[step, c + 2, 0, plane, rows, :]

        far3 = {}
        if c in (-3, 3):
            far3[c] = [
                pltpu.roll(frame[step, 2, X0 + x, Y0:Y0 + RY, :], (-c) % NZ, axis=1) * jnp.float32(c)
                for x in range(CX)
            ]
        seen = {}

        def nearby_once(plane):
            if plane not in seen:
                seen[plane] = nearby(plane)
            return seen[plane]

        for x in range(CX):
            todo = [a for a in range(-far, far + 1) if (a or beta or c) and wanted(a, x)]
            if not todo:
                continue
            mine0 = frame[step, 0, X0 + x, Y0:Y0 + RY, :]
            base = None
            if beta:
                base = turned[step, 2, 1, X0 + x, Y0:Y0 + RY, :]
                if beta != 1:
                    base = base * jnp.float32(beta)
            if c:
                term = frame[step, 2, X0 + x, Y0:Y0 + RY, :]
                if c != 1:
                    term = term * jnp.float32(c)
                base = term if base is None else base + term
            along = None
            total = None
            for a in todo:
                scale = abs(a)
                if base is None:
                    stretch = first(X0 + x + a) - mine0
                    if scale != 1:
                        stretch = stretch * jnp.float32(scale)
                    if a < 0:
                        stretch = -stretch
                else:
                    there, here = nearby_once(X0 + x + a), base
                    if a:
                        near, mine = first(X0 + x + a), mine0
                        if scale != 1:
                            near, mine = near * jnp.float32(scale), mine * jnp.float32(scale)
                        there = there + near if a > 0 else there - near
                        here = here + mine if a > 0 else here - mine
                    stretch = there - here
                pull = table[places[(a, c)], x] * stretch
                total = pull if total is None else total + pull
                if a:
                    part0 = pull * jnp.float32(scale) if scale != 1 else pull
                    if along is None:
                        along = part0 if a > 0 else -part0
                    else:
                        along = along + part0 if a > 0 else along - part0
            if along is not None:
                force[0][x] = along if force[0][x] is None else force[0][x] + along
            if beta:
                addend = total * jnp.float32(beta) if beta != 1 else total
                force[1][x] = addend if force[1][x] is None else force[1][x] + addend
            if c:
                addend = total * jnp.float32(c) if c != 1 else total
                force[2][x] = addend if force[2][x] is None else force[2][x] + addend

    pairs = [
        (beta, c)
        for c in SHIFTS
        for beta in range(-3, 4)
        if beta * beta + c * c <= 9
    ]
    code = bc[bar].astype(jnp.float32)
    retain = 1.0 - 0.2 * code

    for step in range(STEPS):
        for x in range(CX):
            turn(step, X0 + x, Y0)
        force = [[None] * CX for _ in range(3)]
        for beta, c in pairs:
            if beta <= 0:
                block(step, beta, c, force, "own")
        exchange(step, "wait")
        if step == 0:
            weights_of_halo()
        for plane in (1, 2, 9, 10):
            turn(step, plane, Y0)
        for plane in range(1, 11):
            turn(step, plane, halo)
        for x in range(CX):
            pass
        for beta, c in pairs:
            block(step, beta, c, force, "halo")
        for x in range(CX):
            for comp in range(3):
                pull = force[comp][x]
                if comp == 1:
                    pull = pull * fsign
                last = step == STEPS - 1
                speed = retain * (vel[comp, x] + pull)
                moved = frame[step, comp, X0 + x, Y0:Y0 + RY, :] + jnp.float32(time_step) * speed
                if last:
                    v_out[comp, x] = speed
                    u_out[comp, x] = moved
                else:
                    vel[comp, x] = speed
                    frame[step + 1, comp, X0 + x, Y0:Y0 + RY, :] = moved
        if step + 1 < STEPS:
            exchange(step + 1, "start")
    for step in range(STEPS):
        drain(step)


def local_steps(bars, displace, velocity, bond_low, bond_high, bc_type):
    any_space = pl.BlockSpec(memory_space=pl.ANY)
    vmem = pl.BlockSpec(memory_space=pltpu.VMEM)
    shape = jax.ShapeDtypeStruct(displace.shape, jnp.float32)
    return pl.pallas_call(
        functools.partial(kernel, bars),
        out_shape=(shape, shape),
        in_specs=[any_space] * 5,
        out_specs=(vmem, vmem),
        scratch_shapes=[
            pltpu.VMEM((STEPS, 3, PLANES, ROWS, NZ), jnp.float32),
            pltpu.VMEM((2, PLANES, ROWS, NZ), jnp.int32),
            pltpu.VMEM((3, CX, RY, NZ), jnp.float32),
            pltpu.SMEM((bc_type.shape[0],), jnp.int32),
            pltpu.VMEM((STEPS, 5, 3, PLANES, ROWS, NZ), jnp.float32),
            pltpu.VMEM((2, 6, PLANES, ROWS, NZ), jnp.int32),
            pltpu.VMEM((7, 29, CX, RY, NZ), jnp.float32),
            pltpu.SemaphoreType.DMA((5,)),
            pltpu.SemaphoreType.DMA((STEPS, 16)),
            pltpu.SemaphoreType.DMA((STEPS, 16)),
        ],
        compiler_params=pltpu.CompilerParams(collective_id=0, has_side_effects=True),
        name="peridynamics",
    )(displace, velocity, bond_low, bond_high, bc_type)


def solution(mesh):
    bars = mesh.shape["bar"]
    return jax.shard_map(
        functools.partial(local_steps, bars),
        mesh=mesh,
        in_specs=(
            P(None, "bar", "lat", None),
            P(None, "bar", "lat", None),
            P("bar", "lat", None),
            P("bar", "lat", None),
            P(),
        ),
        out_specs=(P(None, "bar", "lat", None), P(None, "bar", "lat", None)),
        check_vma=False,
    )
```

time: 85.2 us -> 24.5 us (0.29)
  starting transfers between devices: 34.7 us -> 0 us
  waiting for transfers between devices: 26.2 us -> 0 us
  other arithmetic: 21.5 us -> 0 us
  Pallas kernels: 0 us -> 21.4 us
  local copies, waits for them, and re-layouts: 0.92 us -> 2.19 us
    ppermute x12 -> x0, starting transfers between devices: 34.7 us -> none  [the longest x6 24.4 us: with_halo(): lax.ppermute(head, axis, [((i + 1) % count, i) for i in range(ends)])]
    ppermute x12 -> x0, waiting for transfers between devices: 26.2 us -> none  [the longest x6 25.1 us: with_halo(): lax.ppermute(tail, axis, [(i, (i + 1) % count) for i in range(ends)])]
    pallas_call x0 -> x1, Pallas kernels: none -> 21.4 us  [local_steps(): pl.pallas_call(functools.partial(kernel, bars), out_shape=(shape, shape),...]
    mul x54 -> x0, other arithmetic: 11.5 us -> none  [the longest x48 11.4 us: bond_forces(): bond_term = modulus / length * intact * reach_mask * stretch]
    another operation x7 -> x0, other arithmetic: 8.08 us -> none  [the longest x6 7.31 us: bond_forces(): return jnp.stack([force_x, force_y, force_z])]
    unnamed x10 -> x4, local copies, waits for them, and re-layouts: 0.04 us -> 2.19 us
    slice x5 -> x0, local copies, waits for them, and re-layouts: 0.88 us -> none  [the longest x1 0.8 us: with_halo(): head = lax.slice_in_dim(cells, 0, width, axis=dim)]
  transfers between devices with their start and end apart: 12 -> 0, of which waited for: 6 -> 0; matrix products, arithmetic and copies ran while one was open for 2% -> 0% of each run, Pallas kernels for 0% -> 0%
where the time goes in v1:
time: 24.5 us; the launch traced here: 24.2 us
  Pallas kernels  21.4 us (87%)
  local copies, waits for them, and re-layouts  2.19 us (9%)
  between operations  0.65 us (3%)
    pallas_call x1, Pallas kernels, local_steps(): pl.pallas_call(functools.partial(kernel, bars), out_shape=(shape, shape),...  21.4 us
    unnamed x4, local copies, waits for them, and re-layouts  2.19 us

profile of v1, /device:TPU:24, one launch (start us, length us, event | category | flops | bytes accessed | tf_op | source)
XLA Modules:
  0.0 24.2 jit_solution(9484647973750509546)
XLA Ops:
  0.6 21.4 %peridynamics.1 = (f32[3,6,8,128]{3,2,1,0:T(8,128)}, f32[3,6,8,128]{3,2,1,0:T(8,128)}) custom-call(f32[3,6,8,128]{3,2,1,0:T(8,128)} %u_hbm.1, f32[3,6,8,128]{3,2,1,0:T(8,128)} %v_hbm.1, s32[6,8,128]{2,1,0:T(8,128)} %low_hbm.1, s32[6,8,128]{2,1,0:T(8,128)} %high_hbm.1, s32[128]{0:T(128)} %bc_hbm.1), custom_call_target="tpu_custom_call" | custom-call | tf_op jit(solution)/shard_map/peridynamics/pallas_call | solution.py:475
  22.0 0.0 copy-start
  22.0 1.6 %copy.9 = f32[3,6,8,128]{3,2,1,0:T(8,128)} copy(f32[3,6,8,128]{3,2,1,0:T(8,128)} %get-tuple-element.4) | data formatting | bytes 147456
  23.6 0.0 copy-done
  23.6 0.6 %copy.10 = f32[3,6,8,128]{3,2,1,0:T(8,128)} copy(f32[3,6,8,128]{3,2,1,0:T(8,128)S(1)} %copy-done) | data formatting | bytes 147456
Async XLA Ops:
  22.0 1.6 %copy-start = (f32[3,6,8,128]{3,2,1,0:T(8,128)S(1)}, f32[3,6,8,128]{3,2,1,0:T(8,128)}, u32[]{:S(2)}) copy-start(f32[3,6,8,128]{3,2,1,0:T(8,128)} %get-tuple-element.5) | copy-start | bytes 221188

commit v2 on v1

--- a/solution.py
+++ b/solution.py
@@ -457,8 +457,8 @@
                 speed = retain * (vel[comp, x] + pull)
                 moved = frame[step, comp, X0 + x, Y0:Y0 + RY, :] + jnp.float32(time_step) * speed
                 if last:
-                    v_out[comp, x] = speed
-                    u_out[comp, x] = moved
+                    v_out[comp, x] = 0.5 * speed
+                    u_out[comp, x] = frame[step, comp, X0 + x, Y0:Y0 + RY, :]
                 else:
                     vel[comp, x] = speed
                     frame[step + 1, comp, X0 + x, Y0:Y0 + RY, :] = moved
@@ -472,11 +472,10 @@
     any_space = pl.BlockSpec(memory_space=pl.ANY)
     vmem = pl.BlockSpec(memory_space=pltpu.VMEM)
     shape = jax.ShapeDtypeStruct(displace.shape, jnp.float32)
-    return pl.pallas_call(
+    base, half = pl.pallas_call(
         functools.partial(kernel, bars),
-        out_shape=(shape, shape),
+        out_shape=(pltpu.VMEM(displace.shape, jnp.float32), pltpu.VMEM(displace.shape, jnp.float32)),
         in_specs=[any_space] * 5,
-        out_specs=(vmem, vmem),
         scratch_shapes=[
             pltpu.VMEM((STEPS, 3, PLANES, ROWS, NZ), jnp.float32),
             pltpu.VMEM((2, PLANES, ROWS, NZ), jnp.int32),
@@ -492,6 +491,7 @@
         compiler_params=pltpu.CompilerParams(collective_id=0, has_side_effects=True),
         name="peridynamics",
     )(displace, velocity, bond_low, bond_high, bc_type)
+    return base + half, half + half
 
 
 def solution(mesh):

time: 24.5 us -> 22.3 us (0.910)
  local copies, waits for them, and re-layouts: 2.19 us -> 0 us
  Pallas kernels: 21.4 us -> 20.7 us
  other arithmetic: 0 us -> 0.67 us
    unnamed x4 -> x0, local copies, waits for them, and re-layouts: 2.19 us -> none
    add x0 -> x1, other arithmetic: none -> 0.67 us  [local_steps(): return (base + half, half + half)]
    pallas_call x1, Pallas kernels: 21.4 us -> 20.7 us  [local_steps(): pl.pallas_call(functools.partial(kernel, bars), out_shape=(pltpu.VMEM(dis...]
where the time goes in v2:
time: 22.3 us; the launch traced here: 22 us
  Pallas kernels  20.7 us (93%)
  other arithmetic  0.67 us (3%)
  between operations  0.64 us (3%)
    pallas_call x1, Pallas kernels, local_steps(): pl.pallas_call(functools.partial(kernel, bars), out_shape=(pltpu.VMEM(dis...  20.7 us
    add x1, other arithmetic, local_steps(): return (base + half, half + half)  0.67 us

profile of v2, /device:TPU:24, one launch (start us, length us, event | category | flops | bytes accessed | tf_op | source)
XLA Modules:
  0.0 22.0 jit_solution(3688378282309528752)
XLA Ops:
  0.6 20.7 %peridynamics.1 = (f32[3,6,8,128]{3,2,1,0:T(8,128)S(1)}, f32[3,6,8,128]{3,2,1,0:T(8,128)S(1)}) custom-call(f32[3,6,8,128]{3,2,1,0:T(8,128)} %u_hbm.1, f32[3,6,8,128]{3,2,1,0:T(8,128)} %v_hbm.1, s32[6,8,128]{2,1,0:T(8,128)} %low_hbm.1, s32[6,8,128]{2,1,0:T(8,128)} %high_hbm.1, s32[128]{0:T(128)} %bc_hbm.1), custom_call_target="tpu_custom_call" | custom-call | tf_op jit(solution)/shard_map/peridynamics/pallas_call | solution.py:475
  21.3 0.7 %fusion = (f32[3,6,8,128]{3,2,1,0:T(8,128)}, f32[3,6,8,128]{3,2,1,0:T(8,128)}) fusion(f32[3,6,8,128]{3,2,1,0:T(8,128)S(1)} %get-tuple-element.4, f32[3,6,8,128]{3,2,1,0:T(8,128)S(1)} %get-tuple-element.5), kind=kLoop, calls=%fused_computation | loop fusion | flops 36864 | bytes 294912 | tf_op jit(solution)/shard_map/add | solution.py:494

commit v3 on v0

v3 whole, which is shorter than its diff:
```python
import functools

import jax
import jax.numpy as jnp
from jax import lax
from jax.experimental import pallas as pl
from jax.experimental.pallas import tpu as pltpu
from jax.sharding import PartitionSpec as P

STEPS = 2
modulus = 0.1
time_step = 0.5
MESH = pl.DeviceIdType.MESH

CX, RY, NZ = 6, 8, 128
PLANES, ROWS = 3 * CX + 5, 3 * RY
X0, Y0 = CX, RY
OWN = slice(Y0, Y0 + RY)
F32 = jnp.float32


def bond_offsets():
    found = []
    for a in range(-3, 4):
        for b in range(-3, 4):
            for c in range(-3, 4):
                square = a * a + b * b + c * c
                if square == 0 or square > 9:
                    continue
                if a > 0 or (a == 0 and b > 0) or (a == 0 and b == 0 and c > 0):
                    found.append((a, b, c))
    return found


BONDS = bond_offsets()
NUMBER = {xi: k for k, xi in enumerate(BONDS)}
TURNS = (-2, -1, 1, 2)


def flag_of(xi):
    k = NUMBER[xi]
    return (0, 1 << k) if k < 31 else (1, 1 << (k - 31))


def bits_where(test):
    words = [0, 0]
    for xi in BONDS:
        if test(*xi):
            word, bit = flag_of(xi)
            words[word] |= bit
    return words


def disc(b):
    return [(a, c) for c in range(-3, 4) for a in range(-3, 4) if a * a + b * b + c * c <= 9]


PLACE = {abs(b): {ac: n for n, ac in enumerate(disc(b))} for b in range(4)}
PAIRS = [(b, c) for c in range(-3, 4) for b in range(-3, 4) if b * b + c * c <= 9]


def reach(b, c):
    return max(a for a in range(4) if a * a + b * b + c * c <= 9)


def strength(a, b, c):
    return time_step * (modulus / float(a * a + b * b + c * c) ** 1.5)


def combine(terms):
    terms = sorted(terms, key=lambda kv: isinstance(kv[0], (int, float)) and kv[0] < 0)
    out = None
    for k, v in terms:
        if not isinstance(k, (int, float)):
            out = v * k if out is None else out + v * k
            continue
        if k == 0:
            continue
        w = v if abs(k) == 1 else v * F32(abs(k))
        if out is None:
            out = w if k > 0 else -w
        else:
            out = out + w if k > 0 else out - w
    return out


def copies(side, refs, sems, bar, lat):
    u, v, flags = refs
    send, recv = sems

    def rows(ref, lead, src, dst, n):
        here = pl.ds(2 * RY - n - side * (RY - n), n)
        there = pl.ds(RY - n + side * (RY + n), n)
        return ref.at[lead, src, here], ref.at[lead, dst, there]

    def tile(ref, lead, src, dst):
        return ref.at[lead, src, OWN], ref.at[lead, dst, OWN]

    every = slice(None)
    own = slice(6, 12)
    plan = {
        "over_right": [
            rows(u, every, slice(7, 12), slice(1, 6), 5),
            rows(flags, every, slice(7, 12), slice(1, 6), 5),
        ],
        "right": [
            tile(u, every, slice(7, 12), slice(1, 6)),
            tile(flags, 1, own, slice(0, 6)),
            tile(flags, 0, slice(8, 12), slice(2, 6)),
            tile(u, 0, slice(6, 7), slice(0, 1)),
        ],
        "over_left": [
            rows(u, every, slice(6, 11), slice(12, 17), 5),
            rows(flags, every, slice(6, 9), slice(12, 15), 5),
        ],
        "left": [
            tile(u, every, slice(6, 11), slice(12, 17)),
            tile(flags, every, slice(6, 9), slice(12, 15)),
            tile(u, 0, slice(11, 12), slice(17, 18)),
        ],
        "over": [rows(u, every, own, own, 6), rows(flags, every, own, own, 6)],
        "over_right_v": [rows(v, every, slice(10, 12), slice(4, 6), 2)],
        "right_v": [tile(v, every, slice(10, 12), slice(4, 6)), tile(v, 0, slice(9, 10), slice(3, 4))],
        "over_left_v": [rows(v, every, slice(6, 8), slice(12, 14), 2)],
        "left_v": [tile(v, every, slice(6, 8), slice(12, 14)), tile(v, 0, slice(8, 9), slice(14, 15))],
        "over_v": [rows(v, every, own, own, 3)],
    }
    partner = {
        "right": (bar + 1, lat),
        "left": (bar - 1, lat),
        "over": (bar, 1 - lat),
        "over_right": (bar + 1, 1 - lat),
        "over_left": (bar - 1, 1 - lat),
    }
    made = {}
    slot = 0
    for name, pairs in plan.items():
        made[name] = []
        where = partner[name.removesuffix("_v")]
        for src, dst in pairs:
            made[name].append(
                functools.partial(
                    pltpu.make_async_remote_copy,
                    src_ref=src,
                    dst_ref=dst,
                    send_sem=send.at[slot],
                    recv_sem=recv.at[slot],
                    device_id={"bar": where[0], "lat": where[1]},
                    device_id_type=MESH,
                )
            )
            slot += 1
    return made


def kernel(
    bars,
    u_hbm, v_hbm, low_hbm, high_hbm, bc_hbm,
    base_out, half_out,
    frame, flags, vel, speeds, bc, turned, spun, weight, local, send, recv,
):
    bar, lat = lax.axis_index("bar"), lax.axis_index("lat")
    has_left, has_right = bar > 0, bar < bars - 1
    flat_frame = frame.reshape(STEPS, 3, PLANES * ROWS, NZ)
    flat_flags = flags.reshape(2, PLANES * ROWS, NZ)
    flat_vel = vel.reshape(3, PLANES * ROWS, NZ)
    flat_turned = turned.reshape(STEPS, 5, 3, PLANES * ROWS, NZ)
    flat_spun = spun.reshape(2, 5, PLANES * ROWS, NZ)

    loads = [
        pltpu.make_async_copy(low_hbm, flags.at[0, X0:X0 + CX, OWN], local.at[0]),
        pltpu.make_async_copy(high_hbm, flags.at[1, X0:X0 + CX, OWN], local.at[1]),
        pltpu.make_async_copy(u_hbm, frame.at[0, :, X0:X0 + CX, OWN], local.at[2]),
        pltpu.make_async_copy(v_hbm, vel.at[:, X0:X0 + CX, OWN], local.at[3]),
        pltpu.make_async_copy(bc_hbm, bc, local.at[4]),
    ]
    barrier = pltpu.get_barrier_semaphore()

    def greet(b, l):
        pl.semaphore_signal(barrier, inc=1, device_id={"bar": b, "lat": l}, device_id_type=MESH)

    greet(bar, 1 - lat)

    @pl.when(has_left)
    def _():
        greet(bar - 1, lat)
        greet(bar - 1, 1 - lat)

    @pl.when(has_right)
    def _():
        greet(bar + 1, lat)
        greet(bar + 1, 1 - lat)

    for copy in loads:
        copy.start()

    void = pl.ds(pl.multiple_of(lat * (2 * RY), RY), RY)
    halo = pl.ds(pl.multiple_of((1 - lat) * (2 * RY), RY), RY)
    for step, first, last in ((0, 1, 17), (1, 4, 14)):
        zero = jnp.zeros((last - first, RY, NZ), F32)
        for comp in range(3):
            if comp < 2:
                frame[step, comp, first:last, void, :] = zero
            for c in TURNS:
                turned[step, c + 2, comp, first:last, void, :] = zero
    for word in range(2):
        flags[word, 0:15, void, :] = jnp.full((15, RY, NZ), -1, jnp.int32)
        for c in TURNS:
            spun[word, c + 2, 1:15, void, :] = jnp.full((14, RY, NZ), -1, jnp.int32)

    @pl.when(jnp.logical_not(has_left))
    def _():
        for comp in range(3):
            frame[0, comp, 0:6] = jnp.zeros((6, ROWS, NZ), F32)
            vel[comp, 3:6] = jnp.zeros((3, ROWS, NZ), F32)
        for word in range(2):
            flags[word, 0:6] = jnp.full((6, ROWS, NZ), -1, jnp.int32)

    @pl.when(jnp.logical_not(has_right))
    def _():
        for comp in range(3):
            frame[0, comp, 12:18] = jnp.zeros((6, ROWS, NZ), F32)
            vel[comp, 12:15] = jnp.zeros((3, ROWS, NZ), F32)

    sems = (send, recv)
    refs = (frame.at[0], vel, flags)
    sent = copies(lat, refs, sems, bar, lat)
    got = copies(1 - lat, refs, sems, bar, lat)

    def exchange(names, act):
        for name in names:
            partner = name.removesuffix("_v")
            made = got if act == "wait_recv" and partner.startswith("over") else sent
            if act == "wait_recv":
                there = {"right": has_left, "left": has_right}.get(partner.split("_")[-1])
            else:
                there = {"right": has_right, "left": has_left}.get(partner.split("_")[-1])

            def run():
                for copy in made[name]:
                    getattr(copy(), act)()

            if there is None:
                run()
            else:
                pl.when(there)(run)

    row = lax.broadcasted_iota(jnp.int32, (RY, NZ), 0)
    lane = lax.broadcasted_iota(jnp.int32, (RY, NZ), 1)
    for copy in loads[:2]:
        copy.wait()
    for word in range(2):
        gone = jnp.zeros((RY, NZ), jnp.int32)
        for t in range(3):
            under = bits_where(lambda a, b, c: b < -t)[word]
            above = bits_where(lambda a, b, c: b > t)[word]
            cut = jnp.where(lat == 0, jnp.int32(under), jnp.int32(above))
            gone = jnp.where(row == t + lat * (RY - 1 - 2 * t), cut, gone)
        for t in range(3):
            under = bits_where(lambda a, b, c: c < -t)[word]
            above = bits_where(lambda a, b, c: c > t)[word]
            gone = jnp.where(lane == t, gone | jnp.int32(under), gone)
            gone = jnp.where(lane == NZ - 1 - t, gone | jnp.int32(above), gone)
        for x in range(CX):
            flags[word, X0 + x, OWN, :] = flags[word, X0 + x, OWN, :] | gone

    @pl.when(jnp.logical_not(has_right))
    def _():
        for x in range(3, CX):
            beyond = bits_where(lambda a, b, c: x + a >= CX)
            for word in range(2):
                flags[word, X0 + x, OWN, :] = flags[word, X0 + x, OWN, :] | jnp.int32(beyond[word])

    for copy in loads[2:]:
        copy.wait()
    sign = 1 - 2 * lat
    fsign = sign.astype(F32)
    edge_row = {d: Y0 + RY - 1 + d - lat * (RY - 1 + 2 * d) for d in (1, 2, 3)}

    class Tile:
        def __init__(self, plane):
            self.plane = plane

        def get(self, ref, flat, lead, a, b):
            return ref[(*lead, X0 + self.plane + a, pl.ds(Y0 + b, RY), slice(None))]

        def put(self, ref, flat, lead, value):
            ref[(*lead, X0 + self.plane, OWN, slice(None))] = value

    class Row:
        def __init__(self, plane, d):
            self.plane, self.d = plane, d

        def at(self, a, b):
            return pl.ds(edge_row[self.d] + ((X0 + self.plane + a) * ROWS + b), RY, stride=ROWS)

        def get(self, ref, flat, lead, a, b):
            return flat[(*lead, self.at(a, b), slice(None))]

        def put(self, ref, flat, lead, value):
            flat[(*lead, self.at(0, 0), slice(None))] = value

    def spin(plane, rows, words=(0, 1)):
        for word in words:
            held = flags[word, plane, rows, :]
            for c in TURNS:
                spun[word, c + 2, plane, rows, :] = pltpu.roll(held, (-c) % NZ, axis=1)

    def turn(step, plane, rows):
        for comp in range(3):
            held = frame[step, comp, plane, rows, :]
            for c in TURNS:
                moved = pltpu.roll(held, (-c) % NZ, axis=1)
                turned[step, c + 2, comp, plane, rows, :] = combine([(c if comp == 2 else 1, moved)])

    def put_weight(xi, back, planes):
        a, b, c = xi
        word, bit = flag_of(xi)
        a1, b1, c1 = (-a, -b, -c) if back else xi
        place = PLACE[abs(b1)][(a1, c1)]
        for x in planes:
            if not back:
                held = flags[word, X0 + x, OWN, :]
            elif c == 0:
                held = flags[word, X0 + x + a1, Y0 + b1:Y0 + b1 + RY, :]
            elif c == 3:
                held = pltpu.roll(flags[word, X0 + x, OWN, :], 3, axis=1)
            else:
                held = spun[word, c1 + 2, X0 + x + a1, Y0 + b1:Y0 + b1 + RY, :]
            weight[b1 + 3, place, x] = jnp.where((held & jnp.int32(bit)) == 0, F32(strength(*xi)), F32(0.0))

    def add_terms(step, b, shift, factor, c, tasks):
        seen = {}
        for group, todo, force, want, table in tasks:
            if 0 not in want:
                todo = todo if (b or c) and (1 not in want or b or 2 in want) else []
            elif want == (0,):
                todo = [a for a in todo if a]
            todo = [a for a in todo if a or b or c]
            if not todo:
                continue

            def fetch(comp, a):
                if c == 0:
                    return group.get(frame, flat_frame, (step, comp), a, shift)
                return group.get(turned, flat_turned, (step, c + 2, comp), a, shift)

            def mine(comp):
                return group.get(frame, flat_frame, (step, comp), 0, 0)

            def nearby(a):
                key = (group.plane + a, isinstance(group, Row) and group.d)
                if key not in seen:
                    terms = []
                    if abs(c) == 3:
                        terms.append((c, pltpu.roll(mine(2), (-c) % NZ, axis=1)))
                    elif c:
                        terms.append((1, fetch(2, a)))
                    if b:
                        terms.append((factor, fetch(1, a)))
                    seen[key] = combine(terms)
                return seen[key]

            def kept(a, value):
                if table is not None:
                    return table[PLACE[abs(b)][(a, c)], group.plane] * value
                if (a, b, c) in NUMBER:
                    word, bit = flag_of((a, b, c))
                    held = group.get(flags, flat_flags, (word,), 0, 0)
                else:
                    word, bit = flag_of((-a, -b, -c))
                    if c == 0:
                        held = group.get(flags, flat_flags, (word,), a, b)
                    elif c == -3:
                        held = pltpu.roll(group.get(flags, flat_flags, (word,), 0, 0), 3, axis=1)
                    else:
                        held = group.get(spun, flat_spun, (word, c + 2), a, b)
                return jnp.where((held & jnp.int32(bit)) == 0, value, F32(0.0))

            mine0 = mine(0) if any(todo) else None
            base = combine([(factor, mine(1))] * bool(b) + [(c, mine(2))] * bool(c))
            pulls = {}
            for a in todo:
                if base is None:
                    pulls[a] = kept(a, fetch(0, a) - mine0)
                    continue
                there, here = nearby(a), base
                if a:
                    there = combine([(1, there), (a, fetch(0, a))])
                    here = combine([(1, here), (a, mine0)])
                pulls[a] = kept(a, there - here)
            total, along = None, None
            for size in range(4):
                plus, minus = pulls.get(size), pulls.get(-size) if size else None
                if plus is None and minus is None:
                    continue
                k = 1.0 if table is not None else strength(size, b, c)
                if base is None:
                    both = combine([(1, v) for v in (plus, minus) if v is not None])
                    along = combine([(1, along)] * (along is not None) + [(k * size * size, both)])
                    continue
                both = combine([(1, v) for v in (plus, minus) if v is not None])
                total = combine([(1, total)] * (total is not None) + [(k, both)])
                if size and 0 in want:
                    if plus is None:
                        term = (-k * size, minus)
                    elif minus is None:
                        term = (k * size, plus)
                    else:
                        term = (k * size, plus - minus)
                    along = combine([(1, along)] * (along is not None) + [term])
            for comp, k, value in ((0, 1, along), (1, factor, total), (2, c, total)):
                if comp not in want or value is None or (comp == 1 and not b) or (comp == 2 and not c):
                    continue
                force[comp] = combine([(1, force[comp])] * (force[comp] is not None) + [(k, value)])

    retain = {}
    for key, where in (("left", jnp.maximum(bar - 1, 0)), ("own", bar), ("right", jnp.minimum(bar + 1, bars - 1))):
        retain[key] = 1.0 - 0.2 * bc[where].astype(F32)

    def retain_of(group):
        if isinstance(group, Tile):
            return retain["left" if group.plane < 0 else "own" if group.plane < CX else "right"]
        plane = row + group.plane
        return jnp.where(plane < 0, retain["left"], jnp.where(plane < CX, retain["own"], retain["right"]))

    def advance(group, force, want=(0, 1, 2)):
        keep = retain_of(group)
        for comp in want:
            speed = keep * (group.get(vel, flat_vel, (comp,), 0, 0) + force[comp])
            moved = group.get(frame, flat_frame, (0, comp), 0, 0) + F32(time_step) * speed
            if isinstance(group, Tile) and 0 <= group.plane < CX:
                speeds[comp, group.plane] = speed
            group.put(frame, flat_frame, (1, comp), moved)
            far = (group.plane in (-3, 8)) if isinstance(group, Tile) else group.d == 3
            if not far:
                for c in TURNS:
                    value = pltpu.roll(moved, (-c) % NZ, axis=1)
                    group.put(turned, flat_turned, (1, c + 2, comp), combine([(c if comp == 2 else 1, value)]))

    def blank():
        return [None, None, None]

    def span(b, c):
        far = reach(b, c)
        return range(-far, far + 1)

    own = [Tile(x) for x in range(CX)]
    force = [blank() for _ in range(CX)]
    every = (0, 1, 2)

    def own_terms(step, beta, c, chosen, pulls):
        shift, factor = (sign * beta, fsign * F32(beta)) if beta else (0, 0)
        table = weight.at[3 + shift]
        tasks = [
            (own[x], [a for a in span(beta, c) if chosen(x, x + a)], pulls[x], every, table) for x in range(CX)
        ]
        add_terms(step, beta, shift, factor, c, tasks)

    def outer(groups_wants, chosen=lambda group, a: True):
        made = [(entry[0], entry[2] if len(entry) > 2 else blank(), entry[1]) for entry in groups_wants]
        for b, c in PAIRS:
            add_terms(
                0, b, b, b, c,
                [(group, [a for a in span(b, c) if chosen(group, a)], pull, want, None) for group, pull, want in made],
            )
        return made

    def advance_all(made):
        for group, pull, want in made:
            advance(group, pull, want)

    for x in range(CX):
        spin(X0 + x, OWN)
        turn(0, X0 + x, OWN)
    for xi in BONDS:
        put_weight(xi, False, range(CX))
    for xi in BONDS:
        if xi[1] == 0:
            put_weight(xi, True, range(xi[0], CX))
    for side in range(2):

        @pl.when(lat == side)
        def _():
            for xi in BONDS:
                if xi[1] * (1 - 2 * side) > 0:
                    put_weight(xi, True, range(xi[0], CX))

    for beta, c in PAIRS:
        if beta <= 0:
            own_terms(0, beta, c, lambda x, q: 0 <= q < CX, force)

    pl.semaphore_wait(barrier, 1 + 2 * has_left.astype(jnp.int32) + 2 * has_right.astype(jnp.int32))
    exchange(tuple(sent), "start")

    exchange(("left", "over_left"), "wait_recv")
    for plane in range(12, 17):
        turn(0, plane, OWN)
        turn(0, plane, halo)
    for plane in range(12, 15):
        spin(plane, OWN)
        spin(plane, halo)
    for b, c in PAIRS:
        add_terms(0, b, b, b, c, [
            (own[x], [a for a in span(b, c) if x + a >= CX], force[x], every, weight.at[3 + b]) for x in range(CX)
        ])
    right_tiles = [(Tile(6), every, blank()), (Tile(7), every, blank()), (Tile(8), (0,), blank())]
    right_rows = [(Row(6, d), every, blank()) for d in (1, 2)]
    outer(right_tiles, lambda group, a: group.plane + a >= CX)
    for entry in right_rows:
        outer([entry], lambda group, a: a >= 0)

    exchange(("over",), "wait_recv")
    for x in range(CX):
        spin(X0 + x, halo)
        turn(0, X0 + x, halo)
    for side in range(2):

        @pl.when(lat == side)
        def _():
            for xi in BONDS:
                if xi[1] * (1 - 2 * side) < 0:
                    put_weight(xi, True, range(xi[0], CX))

    for beta, c in PAIRS:
        if beta > 0:
            own_terms(0, beta, c, lambda x, q: 0 <= q < CX, force)
    for x in range(3, CX):
        advance(own[x], force[x])
    made = outer(right_tiles, lambda group, a: group.plane + a < CX)
    exchange(("left_v",), "wait_recv")
    advance_all(made)
    made = []
    for entry in right_rows:
        made += outer([entry], lambda group, a: a < 0)
    exchange(("over_v", "over_left_v"), "wait_recv")
    advance_all(made)
    third = blank()
    outer([(Row(0, 3), (1,), third)], lambda group, a: a >= 0)
    again = [blank() for _ in range(CX)]

    def early(x, q):
        return x >= 3 and q >= 3

    for beta, c in PAIRS:
        if beta <= 0:
            own_terms(1, beta, c, early, again)

    exchange(("right", "over_right"), "wait_recv")
    for plane in range(1, 6):
        spin(plane, OWN)
        turn(0, plane, OWN)
        spin(plane, halo)
        turn(0, plane, halo)
    for xi in BONDS:
        put_weight(xi, True, range(min(xi[0], CX)))
    for beta, c in PAIRS:
        own_terms(0, beta, c, lambda x, q: q < 0, force)
    for x in range(3):
        advance(own[x], force[x])
    made = outer([(Tile(-3), (0,)), (Tile(-2), every), (Tile(-1), every)])
    exchange(("right_v", "over_right_v"), "wait_recv")
    advance_all(made)
    made = outer([(Row(-2, 1), every)]) + outer([(Row(-2, 2), every)])
    made += outer([(Row(0, 3), (1,), third)], lambda group, a: a < 0)
    advance_all(made)

    for beta, c in PAIRS:
        own_terms(1, beta, c, (lambda x, q: not early(x, q)) if beta <= 0 else (lambda x, q: True), again)
    for x in range(CX):
        for comp in range(3):
            speed = retain["own"] * (speeds[comp, x] + again[x][comp])
            half_out[comp, x] = F32(time_step) * speed
            base_out[comp, x] = frame[1, comp, X0 + x, OWN, :]
    exchange(tuple(sent), "wait_send")


def local_steps(bars, displace, velocity, bond_low, bond_high, bc_type):
    any_space = pl.BlockSpec(memory_space=pl.ANY)
    out = pltpu.VMEM(displace.shape, F32)
    base, half = pl.pallas_call(
        functools.partial(kernel, bars),
        out_shape=(out, out),
        in_specs=[any_space] * 5,
        scratch_shapes=[
            pltpu.VMEM((STEPS, 3, PLANES, ROWS, NZ), F32),
            pltpu.VMEM((2, PLANES, ROWS, NZ), jnp.int32),
            pltpu.VMEM((3, PLANES, ROWS, NZ), F32),
            pltpu.VMEM((3, CX, RY, NZ), F32),
            pltpu.SMEM((bc_type.shape[0],), jnp.int32),
            pltpu.VMEM((STEPS, 5, 3, PLANES, ROWS, NZ), F32),
            pltpu.VMEM((2, 5, PLANES, ROWS, NZ), jnp.int32),
            pltpu.VMEM((7, 29, CX, RY, NZ), F32),
            pltpu.SemaphoreType.DMA((5,)),
            pltpu.SemaphoreType.DMA((20,)),
            pltpu.SemaphoreType.DMA((20,)),
        ],
        compiler_params=pltpu.CompilerParams(collective_id=0, has_side_effects=True),
        name="peridynamics",
    )(displace, velocity, bond_low, bond_high, bc_type)
    return base + half, half + half


def solution(mesh):
    bars = mesh.shape["bar"]
    return jax.shard_map(
        functools.partial(local_steps, bars),
        mesh=mesh,
        in_specs=(
            P(None, "bar", "lat", None),
            P(None, "bar", "lat", None),
            P("bar", "lat", None),
            P("bar", "lat", None),
            P(),
        ),
        out_specs=(P(None, "bar", "lat", None), P(None, "bar", "lat", None)),
        check_vma=False,
    )
```

time: 85.2 us -> 19.9 us (0.23)
  starting transfers between devices: 34.7 us -> 0 us
  waiting for transfers between devices: 26.2 us -> 0 us
  other arithmetic: 21.5 us -> 0.67 us
  Pallas kernels: 0 us -> 18.3 us
  local copies, waits for them, and re-layouts: 0.92 us -> 0 us
    ppermute x12 -> x0, starting transfers between devices: 34.7 us -> none  [the longest x6 24.4 us: with_halo(): lax.ppermute(head, axis, [((i + 1) % count, i) for i in range(ends)])]
    ppermute x12 -> x0, waiting for transfers between devices: 26.2 us -> none  [the longest x6 25.1 us: with_halo(): lax.ppermute(tail, axis, [(i, (i + 1) % count) for i in range(ends)])]
    pallas_call x0 -> x1, Pallas kernels: none -> 18.3 us  [local_steps(): pl.pallas_call(functools.partial(kernel, bars), out_shape=(out, out), in_...]
    mul x54 -> x0, other arithmetic: 11.5 us -> none  [the longest x48 11.4 us: bond_forces(): bond_term = modulus / length * intact * reach_mask * stretch]
    another operation x7 -> x0, other arithmetic: 8.08 us -> none  [the longest x6 7.31 us: bond_forces(): return jnp.stack([force_x, force_y, force_z])]
    slice x5 -> x0, local copies, waits for them, and re-layouts: 0.88 us -> none  [the longest x1 0.8 us: with_halo(): head = lax.slice_in_dim(cells, 0, width, axis=dim)]
  transfers between devices with their start and end apart: 12 -> 0, of which waited for: 6 -> 0; matrix products, arithmetic and copies ran while one was open for 2% -> 0% of each run, Pallas kernels for 0% -> 0%
where the time goes in v3:
time: 19.9 us; the launch traced here: 19.6 us
  Pallas kernels  18.3 us (92%)
  other arithmetic  0.67 us (3%)
  between operations  0.64 us (3%)
    pallas_call x1, Pallas kernels, local_steps(): pl.pallas_call(functools.partial(kernel, bars), out_shape=(out, out), in_...  18.3 us
    add x1, other arithmetic, local_steps(): return (base + half, half + half)  0.67 us

profile of v3, /device:TPU:24, one launch (start us, length us, event | category | flops | bytes accessed | tf_op | source)
XLA Modules:
  0.0 19.6 jit_solution(12388356885460705836)
XLA Ops:
  0.6 18.3 %peridynamics.1 = (f32[3,6,8,128]{3,2,1,0:T(8,128)S(1)}, f32[3,6,8,128]{3,2,1,0:T(8,128)S(1)}) custom-call(f32[3,6,8,128]{3,2,1,0:T(8,128)} %u_hbm.1, f32[3,6,8,128]{3,2,1,0:T(8,128)} %v_hbm.1, s32[6,8,128]{2,1,0:T(8,128)} %low_hbm.1, s32[6,8,128]{2,1,0:T(8,128)} %high_hbm.1, s32[128]{0:T(128)} %bc_hbm.1), custom_call_target="tpu_custom_call" | custom-call | tf_op jit(solution)/shard_map/peridynamics/pallas_call | solution.py:581
  18.9 0.7 %fusion = (f32[3,6,8,128]{3,2,1,0:T(8,128)}, f32[3,6,8,128]{3,2,1,0:T(8,128)}) fusion(f32[3,6,8,128]{3,2,1,0:T(8,128)S(1)} %get-tuple-element.4, f32[3,6,8,128]{3,2,1,0:T(8,128)S(1)} %get-tuple-element.5), kind=kLoop, calls=%fused_computation | loop fusion | flops 36864 | bytes 294912 | tf_op jit(solution)/shard_map/add | solution.py:601

commit v4 on v3

--- a/solution.py
+++ b/solution.py
@@ -15,6 +15,7 @@
 CX, RY, NZ = 6, 8, 128
 PLANES, ROWS = 3 * CX + 5, 3 * RY
 X0, Y0 = CX, RY
+LINE = 25
 OWN = slice(Y0, Y0 + RY)
 F32 = jnp.float32
 
@@ -56,7 +57,13 @@
 
 
 PLACE = {abs(b): {ac: n for n, ac in enumerate(disc(b))} for b in range(4)}
-PAIRS = [(b, c) for c in range(-3, 4) for b in range(-3, 4) if b * b + c * c <= 9]
+PAIRS = [
+    pair
+    for c in range(0, 4)
+    for b in range(-3, 4)
+    if b * b + c * c <= 9 and (c > 0 or b >= 0)
+    for pair in dict.fromkeys(((b, c), (-b, -c)))
+]
 
 
 def reach(b, c):
@@ -157,15 +164,13 @@
     bars,
     u_hbm, v_hbm, low_hbm, high_hbm, bc_hbm,
     base_out, half_out,
-    frame, flags, vel, speeds, bc, turned, spun, weight, local, send, recv,
+    frame, flags, vel, speeds, bc, lines, marks, turned, spun, weight, local, send, recv,
 ):
     bar, lat = lax.axis_index("bar"), lax.axis_index("lat")
     has_left, has_right = bar > 0, bar < bars - 1
     flat_frame = frame.reshape(STEPS, 3, PLANES * ROWS, NZ)
-    flat_flags = flags.reshape(2, PLANES * ROWS, NZ)
     flat_vel = vel.reshape(3, PLANES * ROWS, NZ)
     flat_turned = turned.reshape(STEPS, 5, 3, PLANES * ROWS, NZ)
-    flat_spun = spun.reshape(2, 5, PLANES * ROWS, NZ)
 
     loads = [
         pltpu.make_async_copy(low_hbm, flags.at[0, X0:X0 + CX, OWN], local.at[0]),
@@ -195,7 +200,8 @@
         copy.start()
 
     void = pl.ds(pl.multiple_of(lat * (2 * RY), RY), RY)
-    halo = pl.ds(pl.multiple_of((1 - lat) * (2 * RY), RY), RY)
+    halo_start = pl.multiple_of((1 - lat) * (2 * RY), RY)
+    halo = pl.ds(halo_start, RY)
     for step, first, last in ((0, 1, 17), (1, 4, 14)):
         zero = jnp.zeros((last - first, RY, NZ), F32)
         for comp in range(3):
@@ -281,7 +287,7 @@
         def __init__(self, plane):
             self.plane = plane
 
-        def get(self, ref, flat, lead, a, b):
+        def get(self, ref, lead, a, b):
             return ref[(*lead, X0 + self.plane + a, pl.ds(Y0 + b, RY), slice(None))]
 
         def put(self, ref, flat, lead, value):
@@ -291,27 +297,44 @@
         def __init__(self, plane, d):
             self.plane, self.d = plane, d
 
-        def at(self, a, b):
-            return pl.ds(edge_row[self.d] + ((X0 + self.plane + a) * ROWS + b), RY, stride=ROWS)
-
-        def get(self, ref, flat, lead, a, b):
-            return flat[(*lead, self.at(a, b), slice(None))]
+        def get(self, ref, lead, a, b):
+            at = pl.ds(edge_row[self.d] * LINE + ((X0 + self.plane + a) + b * LINE), RY)
+            if ref is frame:
+                return lines[2, lead[1], at, :]
+            if ref is turned:
+                return lines[lead[1], lead[2], at, :]
+            if ref is flags:
+                return marks[lead[0], 2, at, :]
+            if ref is spun:
+                return marks[lead[0], lead[1], at, :]
+            return flat_vel[(*lead, self.strided(), slice(None))]
+
+        def strided(self):
+            return pl.ds(edge_row[self.d] + (X0 + self.plane) * ROWS, RY, stride=ROWS)
 
         def put(self, ref, flat, lead, value):
-            flat[(*lead, self.at(0, 0), slice(None))] = value
-
-    def spin(plane, rows, words=(0, 1)):
-        for word in words:
+            flat[(*lead, self.strided(), slice(None))] = value
+
+    def line(plane, rows):
+        return pl.ds((Y0 * LINE if rows is OWN else halo_start * LINE) + plane, RY, stride=LINE)
+
+    def spin(plane, rows, turns=(-2, -1, 0, 1, 2)):
+        for word in range(2):
             held = flags[word, plane, rows, :]
-            for c in TURNS:
-                spun[word, c + 2, plane, rows, :] = pltpu.roll(held, (-c) % NZ, axis=1)
-
-    def turn(step, plane, rows):
+            for c in turns:
+                moved = pltpu.roll(held, (-c) % NZ, axis=1) if c else held
+                marks[word, c + 2, line(plane, rows), :] = moved
+                if c:
+                    spun[word, c + 2, plane, rows, :] = moved
+
+    def turn(plane, rows, turns=(-2, -1, 0, 1, 2)):
         for comp in range(3):
-            held = frame[step, comp, plane, rows, :]
-            for c in TURNS:
-                moved = pltpu.roll(held, (-c) % NZ, axis=1)
-                turned[step, c + 2, comp, plane, rows, :] = combine([(c if comp == 2 else 1, moved)])
+            held = frame[0, comp, plane, rows, :]
+            for c in turns:
+                moved = combine([(c if comp == 2 else 1, pltpu.roll(held, (-c) % NZ, axis=1))]) if c else held
+                lines[c + 2, comp, line(plane, rows), :] = moved
+                if c:
+                    turned[0, c + 2, comp, plane, rows, :] = moved
 
     def put_weight(xi, back, planes):
         a, b, c = xi
@@ -329,8 +352,14 @@
                 held = spun[word, c1 + 2, X0 + x + a1, Y0 + b1:Y0 + b1 + RY, :]
             weight[b1 + 3, place, x] = jnp.where((held & jnp.int32(bit)) == 0, F32(strength(*xi)), F32(0.0))
 
+    heres = {}
+
     def add_terms(step, b, shift, factor, c, tasks):
         seen = {}
+        opposite = (step, -b, -c)
+        for key in list(heres):
+            if key[:3] != opposite:
+                del heres[key]
         for group, todo, force, want, table in tasks:
             if 0 not in want:
                 todo = todo if (b or c) and (1 not in want or b or 2 in want) else []
@@ -342,11 +371,11 @@
 
             def fetch(comp, a):
                 if c == 0:
-                    return group.get(frame, flat_frame, (step, comp), a, shift)
-                return group.get(turned, flat_turned, (step, c + 2, comp), a, shift)
+                    return group.get(frame, (step, comp), a, shift)
+                return group.get(turned, (step, c + 2, comp), a, shift)
 
             def mine(comp):
-                return group.get(frame, flat_frame, (step, comp), 0, 0)
+                return group.get(frame, (step, comp), 0, 0)
 
             def nearby(a):
                 key = (group.plane + a, isinstance(group, Row) and group.d)
@@ -366,36 +395,42 @@
                     return table[PLACE[abs(b)][(a, c)], group.plane] * value
                 if (a, b, c) in NUMBER:
                     word, bit = flag_of((a, b, c))
-                    held = group.get(flags, flat_flags, (word,), 0, 0)
+                    held = group.get(flags, (word,), 0, 0)
                 else:
                     word, bit = flag_of((-a, -b, -c))
                     if c == 0:
-                        held = group.get(flags, flat_flags, (word,), a, b)
+                        held = group.get(flags, (word,), a, b)
                     elif c == -3:
-                        held = pltpu.roll(group.get(flags, flat_flags, (word,), 0, 0), 3, axis=1)
+                        held = pltpu.roll(group.get(flags, (word,), 0, 0), 3, axis=1)
                     else:
-                        held = group.get(spun, flat_spun, (word, c + 2), a, b)
+                        held = group.get(spun, (word, c + 2), a, b)
                 return jnp.where((held & jnp.int32(bit)) == 0, value, F32(0.0))
 
-            mine0 = mine(0) if any(todo) else None
-            base = combine([(factor, mine(1))] * bool(b) + [(c, mine(2))] * bool(c))
+            needs = [a for a in todo if (*opposite, -a, group) not in heres]
+            mine0 = mine(0) if any(needs) else None
+            alone = not b and not c
+            base = combine([(factor, mine(1))] * bool(b) + [(c, mine(2))] * bool(c)) if needs else None
             pulls = {}
             for a in todo:
-                if base is None:
+                if alone:
                     pulls[a] = kept(a, fetch(0, a) - mine0)
                     continue
-                there, here = nearby(a), base
+                there = nearby(a)
                 if a:
                     there = combine([(1, there), (a, fetch(0, a))])
-                    here = combine([(1, here), (a, mine0)])
-                pulls[a] = kept(a, there - here)
+                if a in needs:
+                    here = combine([(1, base), (a, mine0)]) if a else base
+                    heres[(step, b, c, a, group)] = here
+                    pulls[a] = kept(a, there - here)
+                else:
+                    pulls[a] = kept(a, there + heres[(*opposite, -a, group)])
             total, along = None, None
             for size in range(4):
                 plus, minus = pulls.get(size), pulls.get(-size) if size else None
                 if plus is None and minus is None:
                     continue
                 k = 1.0 if table is not None else strength(size, b, c)
-                if base is None:
+                if alone:
                     both = combine([(1, v) for v in (plus, minus) if v is not None])
                     along = combine([(1, along)] * (along is not None) + [(k * size * size, both)])
                     continue
@@ -427,8 +462,8 @@
     def advance(group, force, want=(0, 1, 2)):
         keep = retain_of(group)
         for comp in want:
-            speed = keep * (group.get(vel, flat_vel, (comp,), 0, 0) + force[comp])
-            moved = group.get(frame, flat_frame, (0, comp), 0, 0) + F32(time_step) * speed
+            speed = keep * (group.get(vel, (comp,), 0, 0) + force[comp])
+            moved = group.get(frame, (0, comp), 0, 0) + F32(time_step) * speed
             if isinstance(group, Tile) and 0 <= group.plane < CX:
                 speeds[comp, group.plane] = speed
             group.put(frame, flat_frame, (1, comp), moved)
@@ -470,9 +505,12 @@
         for group, pull, want in made:
             advance(group, pull, want)
 
+    pl.semaphore_wait(barrier, 1 + 2 * has_left.astype(jnp.int32) + 2 * has_right.astype(jnp.int32))
+    exchange(tuple(sent), "start")
+
     for x in range(CX):
         spin(X0 + x, OWN)
-        turn(0, X0 + x, OWN)
+        turn(X0 + x, OWN)
     for xi in BONDS:
         put_weight(xi, False, range(CX))
     for xi in BONDS:
@@ -490,13 +528,10 @@
         if beta <= 0:
             own_terms(0, beta, c, lambda x, q: 0 <= q < CX, force)
 
-    pl.semaphore_wait(barrier, 1 + 2 * has_left.astype(jnp.int32) + 2 * has_right.astype(jnp.int32))
-    exchange(tuple(sent), "start")
-
     exchange(("left", "over_left"), "wait_recv")
     for plane in range(12, 17):
-        turn(0, plane, OWN)
-        turn(0, plane, halo)
+        turn(plane, OWN)
+        turn(plane, halo)
     for plane in range(12, 15):
         spin(plane, OWN)
         spin(plane, halo)
@@ -513,7 +548,7 @@
     exchange(("over",), "wait_recv")
     for x in range(CX):
         spin(X0 + x, halo)
-        turn(0, X0 + x, halo)
+        turn(X0 + x, halo)
     for side in range(2):
 
         @pl.when(lat == side)
@@ -546,12 +581,13 @@
         if beta <= 0:
             own_terms(1, beta, c, early, again)
 
+    exchange(tuple(sent), "wait_send")
     exchange(("right", "over_right"), "wait_recv")
     for plane in range(1, 6):
         spin(plane, OWN)
-        turn(0, plane, OWN)
+        turn(plane, OWN)
         spin(plane, halo)
-        turn(0, plane, halo)
+        turn(plane, halo)
     for xi in BONDS:
         put_weight(xi, True, range(min(xi[0], CX)))
     for beta, c in PAIRS:
@@ -572,7 +608,6 @@
             speed = retain["own"] * (speeds[comp, x] + again[x][comp])
             half_out[comp, x] = F32(time_step) * speed
             base_out[comp, x] = frame[1, comp, X0 + x, OWN, :]
-    exchange(tuple(sent), "wait_send")
 
 
 def local_steps(bars, displace, velocity, bond_low, bond_high, bc_type):
@@ -588,6 +623,8 @@
             pltpu.VMEM((3, PLANES, ROWS, NZ), F32),
             pltpu.VMEM((3, CX, RY, NZ), F32),
             pltpu.SMEM((bc_type.shape[0],), jnp.int32),
+            pltpu.VMEM((5, 3, ROWS * LINE, NZ), F32),
+            pltpu.VMEM((2, 5, ROWS * LINE, NZ), jnp.int32),
             pltpu.VMEM((STEPS, 5, 3, PLANES, ROWS, NZ), F32),
             pltpu.VMEM((2, 5, PLANES, ROWS, NZ), jnp.int32),
             pltpu.VMEM((7, 29, CX, RY, NZ), F32),

time: 19.9 us -> 18.8 us (0.945)
  Pallas kernels: 18.3 us -> 17.3 us
    pallas_call x1, Pallas kernels: 18.3 us -> 17.3 us  [local_steps(): pl.pallas_call(functools.partial(kernel, bars), out_shape=(out, out), in_...]
where the time goes in v4:
time: 18.8 us; the launch traced here: 18.6 us
  Pallas kernels  17.3 us (92%)
  other arithmetic  0.67 us (4%)
  between operations  0.64 us (3%)
    pallas_call x1, Pallas kernels, local_steps(): pl.pallas_call(functools.partial(kernel, bars), out_shape=(out, out), in_...  17.3 us
    add x1, other arithmetic, local_steps(): return (base + half, half + half)  0.67 us

profile of v4, /device:TPU:24, one launch (start us, length us, event | category | flops | bytes accessed | tf_op | source)
XLA Modules:
  0.0 18.6 jit_solution(11792458120365566218)
XLA Ops:
  0.6 17.3 %peridynamics.1 = (f32[3,6,8,128]{3,2,1,0:T(8,128)S(1)}, f32[3,6,8,128]{3,2,1,0:T(8,128)S(1)}) custom-call(f32[3,6,8,128]{3,2,1,0:T(8,128)} %u_hbm.1, f32[3,6,8,128]{3,2,1,0:T(8,128)} %v_hbm.1, s32[6,8,128]{2,1,0:T(8,128)} %low_hbm.1, s32[6,8,128]{2,1,0:T(8,128)} %high_hbm.1, s32[128]{0:T(128)} %bc_hbm.1), custom_call_target="tpu_custom_call" | custom-call | tf_op jit(solution)/shard_map/peridynamics/pallas_call | solution.py:616
  18.0 0.7 %fusion = (f32[3,6,8,128]{3,2,1,0:T(8,128)}, f32[3,6,8,128]{3,2,1,0:T(8,128)}) fusion(f32[3,6,8,128]{3,2,1,0:T(8,128)S(1)} %get-tuple-element.4, f32[3,6,8,128]{3,2,1,0:T(8,128)S(1)} %get-tuple-element.5), kind=kLoop, calls=%fused_computation | loop fusion | flops 36864 | bytes 294912 | tf_op jit(solution)/shard_map/add | solution.py:638

commit v5 on v4

--- a/solution.py
+++ b/solution.py
@@ -89,6 +89,23 @@
         else:
             out = out + w if k > 0 else out - w
     return out
+
+
+SEND_GROUPS = (
+    ("over", "over_v"),
+    ("right", "over_right", "right_v", "over_right_v"),
+    ("left", "over_left", "left_v", "over_left_v"),
+)
+RECV_GROUPS = (
+    ("over",),
+    ("left", "over_left"),
+    ("right", "over_right"),
+    ("over_v",),
+    ("left_v", "over_left_v"),
+    ("right_v", "over_right_v"),
+)
+SEND_SLOT = {name: slot for slot, names in enumerate(SEND_GROUPS) for name in names}
+RECV_SLOT = {name: slot for slot, names in enumerate(RECV_GROUPS) for name in names}
 
 
 def copies(side, refs, sems, bar, lat):
@@ -140,7 +157,6 @@
         "over_left": (bar - 1, 1 - lat),
     }
     made = {}
-    slot = 0
     for name, pairs in plan.items():
         made[name] = []
         where = partner[name.removesuffix("_v")]
@@ -150,13 +166,12 @@
                     pltpu.make_async_remote_copy,
                     src_ref=src,
                     dst_ref=dst,
-                    send_sem=send.at[slot],
-                    recv_sem=recv.at[slot],
+                    send_sem=send.at[SEND_SLOT[name]],
+                    recv_sem=recv.at[RECV_SLOT[name]],
                     device_id={"bar": where[0], "lat": where[1]},
                     device_id_type=MESH,
                 )
             )
-            slot += 1
     return made
 
 
@@ -231,25 +246,45 @@
     sems = (send, recv)
     refs = (frame.at[0], vel, flags)
     sent = copies(lat, refs, sems, bar, lat)
-    got = copies(1 - lat, refs, sems, bar, lat)
-
-    def exchange(names, act):
-        for name in names:
-            partner = name.removesuffix("_v")
-            made = got if act == "wait_recv" and partner.startswith("over") else sent
-            if act == "wait_recv":
-                there = {"right": has_left, "left": has_right}.get(partner.split("_")[-1])
-            else:
-                there = {"right": has_right, "left": has_left}.get(partner.split("_")[-1])
+
+    def when_there(condition, run):
+        if condition is None:
+            run()
+        else:
+            pl.when(condition)(run)
+
+    def send_all():
+        for name, made in sent.items():
+            there = {"right": has_right, "left": has_left}.get(name.removesuffix("_v").split("_")[-1])
 
             def run():
-                for copy in made[name]:
-                    getattr(copy(), act)()
-
-            if there is None:
-                run()
-            else:
-                pl.when(there)(run)
+                for copy in made:
+                    copy().start()
+
+            when_there(there, run)
+
+    def wait_group(names, sem, there):
+        lines_sent = sum(
+            copy.keywords["src_ref"].shape[0] * copy.keywords["src_ref"].shape[1] * copy.keywords["src_ref"].shape[2]
+            if len(copy.keywords["src_ref"].shape) == 4
+            else copy.keywords["src_ref"].shape[0] * copy.keywords["src_ref"].shape[1]
+            for name in names
+            for copy in sent[name]
+        )
+
+        def run():
+            total = lines.at[0, 0, 0:lines_sent]
+            pltpu.make_async_copy(total, total, sem).wait()
+
+        when_there(there, run)
+
+    def received(*names):
+        there = {"right": has_left, "left": has_right}.get(names[0].removesuffix("_v"))
+        wait_group(names, recv.at[RECV_GROUPS.index(names)], there)
+
+    def all_sent():
+        for slot, there in enumerate((None, has_right, has_left)):
+            wait_group(SEND_GROUPS[slot], send.at[slot], there)
 
     row = lax.broadcasted_iota(jnp.int32, (RY, NZ), 0)
     lane = lax.broadcasted_iota(jnp.int32, (RY, NZ), 1)
@@ -506,7 +541,7 @@
             advance(group, pull, want)
 
     pl.semaphore_wait(barrier, 1 + 2 * has_left.astype(jnp.int32) + 2 * has_right.astype(jnp.int32))
-    exchange(tuple(sent), "start")
+    send_all()
 
     for x in range(CX):
         spin(X0 + x, OWN)
@@ -528,7 +563,7 @@
         if beta <= 0:
             own_terms(0, beta, c, lambda x, q: 0 <= q < CX, force)
 
-    exchange(("left", "over_left"), "wait_recv")
+    received("left", "over_left")
     for plane in range(12, 17):
         turn(plane, OWN)
         turn(plane, halo)
@@ -545,7 +580,7 @@
     for entry in right_rows:
         outer([entry], lambda group, a: a >= 0)
 
-    exchange(("over",), "wait_recv")
+    received("over")
     for x in range(CX):
         spin(X0 + x, halo)
         turn(X0 + x, halo)
@@ -563,12 +598,12 @@
     for x in range(3, CX):
         advance(own[x], force[x])
     made = outer(right_tiles, lambda group, a: group.plane + a < CX)
-    exchange(("left_v",), "wait_recv")
+    received("left_v", "over_left_v")
     advance_all(made)
     made = []
     for entry in right_rows:
         made += outer([entry], lambda group, a: a < 0)
-    exchange(("over_v", "over_left_v"), "wait_recv")
+    received("over_v")
     advance_all(made)
     third = blank()
     outer([(Row(0, 3), (1,), third)], lambda group, a: a >= 0)
@@ -581,8 +616,8 @@
         if beta <= 0:
             own_terms(1, beta, c, early, again)
 
-    exchange(tuple(sent), "wait_send")
-    exchange(("right", "over_right"), "wait_recv")
+    all_sent()
+    received("right", "over_right")
     for plane in range(1, 6):
         spin(plane, OWN)
         turn(plane, OWN)
@@ -595,7 +630,7 @@
     for x in range(3):
         advance(own[x], force[x])
     made = outer([(Tile(-3), (0,)), (Tile(-2), every), (Tile(-1), every)])
-    exchange(("right_v", "over_right_v"), "wait_recv")
+    received("right_v", "over_right_v")
     advance_all(made)
     made = outer([(Row(-2, 1), every)]) + outer([(Row(-2, 2), every)])
     made += outer([(Row(0, 3), (1,), third)], lambda group, a: a < 0)
@@ -629,8 +664,8 @@
             pltpu.VMEM((2, 5, PLANES, ROWS, NZ), jnp.int32),
             pltpu.VMEM((7, 29, CX, RY, NZ), F32),
             pltpu.SemaphoreType.DMA((5,)),
-            pltpu.SemaphoreType.DMA((20,)),
-            pltpu.SemaphoreType.DMA((20,)),
+            pltpu.SemaphoreType.DMA((len(SEND_GROUPS),)),
+            pltpu.SemaphoreType.DMA((len(RECV_GROUPS),)),
         ],
         compiler_params=pltpu.CompilerParams(collective_id=0, has_side_effects=True),
         name="peridynamics",

time: 18.8 us -> 18.4 us (0.979)
  Pallas kernels: 17.3 us -> 17 us
    pallas_call x1, Pallas kernels: 17.3 us -> 17 us  [local_steps(): pl.pallas_call(functools.partial(kernel, bars), out_shape=(out, out), in_...]
where the time goes in v5:
time: 18.4 us; the launch traced here: 18.3 us
  Pallas kernels  17 us (92%)
  other arithmetic  0.67 us (4%)
  between operations  0.64 us (3%)
    pallas_call x1, Pallas kernels, local_steps(): pl.pallas_call(functools.partial(kernel, bars), out_shape=(out, out), in_...  17 us
    add x1, other arithmetic, local_steps(): return (base + half, half + half)  0.67 us

profile of v5, /device:TPU:24, one launch (start us, length us, event | category | flops | bytes accessed | tf_op | source)
XLA Modules:
  0.0 18.3 jit_solution(1110725585722401086)
XLA Ops:
  0.6 17.0 %peridynamics.1 = (f32[3,6,8,128]{3,2,1,0:T(8,128)S(1)}, f32[3,6,8,128]{3,2,1,0:T(8,128)S(1)}) custom-call(f32[3,6,8,128]{3,2,1,0:T(8,128)} %u_hbm.1, f32[3,6,8,128]{3,2,1,0:T(8,128)} %v_hbm.1, s32[6,8,128]{2,1,0:T(8,128)} %low_hbm.1, s32[6,8,128]{2,1,0:T(8,128)} %high_hbm.1, s32[128]{0:T(128)} %bc_hbm.1), custom_call_target="tpu_custom_call" | custom-call | tf_op jit(solution)/shard_map/peridynamics/pallas_call | solution.py:651
  17.6 0.7 %fusion = (f32[3,6,8,128]{3,2,1,0:T(8,128)}, f32[3,6,8,128]{3,2,1,0:T(8,128)}) fusion(f32[3,6,8,128]{3,2,1,0:T(8,128)S(1)} %get-tuple-element.4, f32[3,6,8,128]{3,2,1,0:T(8,128)S(1)} %get-tuple-element.5), kind=kLoop, calls=%fused_computation | loop fusion | flops 36864 | bytes 294912 | tf_op jit(solution)/shard_map/add | solution.py:673

commit v6 on v5

--- a/solution.py
+++ b/solution.py
@@ -254,8 +254,26 @@
             pl.when(condition)(run)
 
     def send_all():
-        for name, made in sent.items():
-            there = {"right": has_right, "left": has_left}.get(name.removesuffix("_v").split("_")[-1])
+        even = lax.rem(bar, 2) == 0
+        odd = jnp.logical_not(even)
+        order = (
+            ('over', even),
+            ('over_v', even),
+            ('over_right', None),
+            ('right', None),
+            ('right_v', None),
+            ('over_right_v', None),
+            ('over', odd),
+            ('over_left', None),
+            ('left', None),
+            ('over_v', odd),
+            ('over_left_v', None),
+            ('left_v', None),
+        )
+        for name, there in order:
+            made = sent[name]
+            if there is None:
+                there = {"right": has_right, "left": has_left}.get(name.removesuffix("_v").split("_")[-1])
 
             def run():
                 for copy in made:

time: 18.4 us -> 17.5 us (0.951)
  Pallas kernels: 17 us -> 16 us
    pallas_call x1, Pallas kernels: 17 us -> 16 us  [local_steps(): pl.pallas_call(functools.partial(kernel, bars), out_shape=(out, out), in_...]
where the time goes in v6:
time: 17.5 us; the launch traced here: 17.3 us
  Pallas kernels  16 us (91%)
  other arithmetic  0.67 us (4%)
  between operations  0.64 us (4%)
    pallas_call x1, Pallas kernels, local_steps(): pl.pallas_call(functools.partial(kernel, bars), out_shape=(out, out), in_...  16 us
    add x1, other arithmetic, local_steps(): return (base + half, half + half)  0.67 us

profile of v6, /device:TPU:24, one launch (start us, length us, event | category | flops | bytes accessed | tf_op | source)
XLA Modules:
  0.0 17.3 jit_solution(2873313434727005576)
XLA Ops:
  0.6 16.0 %peridynamics.1 = (f32[3,6,8,128]{3,2,1,0:T(8,128)S(1)}, f32[3,6,8,128]{3,2,1,0:T(8,128)S(1)}) custom-call(f32[3,6,8,128]{3,2,1,0:T(8,128)} %u_hbm.1, f32[3,6,8,128]{3,2,1,0:T(8,128)} %v_hbm.1, s32[6,8,128]{2,1,0:T(8,128)} %low_hbm.1, s32[6,8,128]{2,1,0:T(8,128)} %high_hbm.1, s32[128]{0:T(128)} %bc_hbm.1), custom_call_target="tpu_custom_call" | custom-call | tf_op jit(solution)/shard_map/peridynamics/pallas_call | solution.py:669
  16.7 0.7 %fusion = (f32[3,6,8,128]{3,2,1,0:T(8,128)}, f32[3,6,8,128]{3,2,1,0:T(8,128)}) fusion(f32[3,6,8,128]{3,2,1,0:T(8,128)S(1)} %get-tuple-element.4, f32[3,6,8,128]{3,2,1,0:T(8,128)S(1)} %get-tuple-element.5), kind=kLoop, calls=%fused_computation | loop fusion | flops 36864 | bytes 294912 | tf_op jit(solution)/shard_map/add | solution.py:691

commit v7 on v6

--- a/solution.py
+++ b/solution.py
@@ -117,6 +117,11 @@
         there = pl.ds(RY - n + side * (RY + n), n)
         return ref.at[lead, src, here], ref.at[lead, dst, there]
 
+    def row(ref, lead, src, dst, n):
+        here = pl.ds(2 * RY - n - side * (RY + 1 - 2 * n), 1)
+        there = pl.ds(RY - n + side * (RY - 1 + 2 * n), 1)
+        return ref.at[lead, src, here], ref.at[lead, dst, there]
+
     def tile(ref, lead, src, dst):
         return ref.at[lead, src, OWN], ref.at[lead, dst, OWN]
 
@@ -124,8 +129,12 @@
     own = slice(6, 12)
     plan = {
         "over_right": [
-            rows(u, every, slice(7, 12), slice(1, 6), 5),
-            rows(flags, every, slice(7, 12), slice(1, 6), 5),
+            rows(u, every, slice(8, 12), slice(2, 6), 4),
+            rows(flags, every, slice(8, 12), slice(2, 6), 4),
+            row(u, every, slice(10, 12), slice(4, 6), 5),
+            row(flags, every, slice(10, 12), slice(4, 6), 5),
+            rows(u, every, slice(7, 8), slice(1, 2), 2),
+            rows(flags, every, slice(7, 8), slice(1, 2), 2),
         ],
         "right": [
             tile(u, every, slice(7, 12), slice(1, 6)),
@@ -142,12 +151,12 @@
             tile(flags, every, slice(6, 9), slice(12, 15)),
             tile(u, 0, slice(11, 12), slice(17, 18)),
         ],
-        "over": [rows(u, every, own, own, 6), rows(flags, every, own, own, 6)],
+        "over": [rows(u, every, own, own, 5), rows(flags, every, own, own, 6), row(u, 1, own, own, 6)],
         "over_right_v": [rows(v, every, slice(10, 12), slice(4, 6), 2)],
         "right_v": [tile(v, every, slice(10, 12), slice(4, 6)), tile(v, 0, slice(9, 10), slice(3, 4))],
         "over_left_v": [rows(v, every, slice(6, 8), slice(12, 14), 2)],
         "left_v": [tile(v, every, slice(6, 8), slice(12, 14)), tile(v, 0, slice(8, 9), slice(14, 15))],
-        "over_v": [rows(v, every, own, own, 3)],
+        "over_v": [rows(v, every, own, own, 2), row(v, 1, own, own, 3)],
     }
     partner = {
         "right": (bar + 1, lat),
@@ -199,17 +208,17 @@
     def greet(b, l):
         pl.semaphore_signal(barrier, inc=1, device_id={"bar": b, "lat": l}, device_id_type=MESH)
 
-    greet(bar, 1 - lat)
+    @pl.when(has_right)
+    def _():
+        greet(bar + 1, 1 - lat)
+        greet(bar + 1, lat)
 
     @pl.when(has_left)
     def _():
+        greet(bar - 1, 1 - lat)
         greet(bar - 1, lat)
-        greet(bar - 1, 1 - lat)
-
-    @pl.when(has_right)
-    def _():
-        greet(bar + 1, lat)
-        greet(bar + 1, 1 - lat)
+
+    greet(bar, 1 - lat)
 
     for copy in loads:
         copy.start()

time: 17.5 us -> 17.3 us (0.989)
  no operation moved by 1% of the time
where the time goes in v7:
time: 17.3 us; the launch traced here: 17.2 us
  Pallas kernels  15.9 us (92%)
  other arithmetic  0.67 us (4%)
  between operations  0.64 us (4%)
    pallas_call x1, Pallas kernels, local_steps(): pl.pallas_call(functools.partial(kernel, bars), out_shape=(out, out), in_...  15.9 us
    add x1, other arithmetic, local_steps(): return (base + half, half + half)  0.67 us

profile of v7, /device:TPU:24, one launch (start us, length us, event | category | flops | bytes accessed | tf_op | source)
XLA Modules:
  0.0 17.2 jit_solution(10729298649525741369)
XLA Ops:
  0.6 15.9 %peridynamics.1 = (f32[3,6,8,128]{3,2,1,0:T(8,128)S(1)}, f32[3,6,8,128]{3,2,1,0:T(8,128)S(1)}) custom-call(f32[3,6,8,128]{3,2,1,0:T(8,128)} %u_hbm.1, f32[3,6,8,128]{3,2,1,0:T(8,128)} %v_hbm.1, s32[6,8,128]{2,1,0:T(8,128)} %low_hbm.1, s32[6,8,128]{2,1,0:T(8,128)} %high_hbm.1, s32[128]{0:T(128)} %bc_hbm.1), custom_call_target="tpu_custom_call" | custom-call | tf_op jit(solution)/shard_map/peridynamics/pallas_call | solution.py:678
  16.5 0.7 %fusion = (f32[3,6,8,128]{3,2,1,0:T(8,128)}, f32[3,6,8,128]{3,2,1,0:T(8,128)}) fusion(f32[3,6,8,128]{3,2,1,0:T(8,128)S(1)} %get-tuple-element.4, f32[3,6,8,128]{3,2,1,0:T(8,128)S(1)} %get-tuple-element.5), kind=kLoop, calls=%fused_computation | loop fusion | flops 36864 | bytes 294912 | tf_op jit(solution)/shard_map/add | solution.py:700
